TPU v7x, 32 devices: a whole 2x2x4 slice. The times are simulated.
32 devices in a mesh: dp: 8 (over z, x), mp: 4 (over y, core).
Axes of the slice: x: 2, y: 2, z: 4, core: 2. Of those that a mesh axis runs over, the one named last changes fastest.
Arguments:
- queries: bfloat16 [16, 16, 5120], P('dp', None, 'mp')
- key_value_cache: bfloat16 [128, 2, 128, 1024], P('dp', None, None, 'mp'), may hold values from -6 to 6
- slot_tags: int32 [128], P('dp'), may hold values from 0 to 15, as said below
- span_key_value: bfloat16 [16, 2, 16, 1024], P('dp', None, None, 'mp'), may hold values from -6 to 6
- answer_id: int32 [16], P('dp'), may hold values from 0 to 127
- w_cand: bfloat16 [5120, 128], P('mp')
Outputs:
- attended: bfloat16 [16, 16, 5120], P('dp', None, 'mp')
- chain_score: float32 [16], P('dp')
- answer_tally: float32 [1, 128], P(None, 'dp')
Inputs may be any that keep to these rules, and one draw needn't show every extreme that they name: `slot_tags`: among the 16 blocks of any one index of dp, at most 2 belong to the chains o * 2 to o * 2 + 1 of any one o, and for some o every index of dp holds exactly 2 such blocks. A chain may have no cached block.
All inputs are finite; a program needn't handle non-finite values.
Results may differ from a plain program's by a relative error of at most 0.0075.
Values may be sent and summed in bfloat16 or wider, within the bound.
No kernel may reach another device: no remote copies, remote signals or barrier semaphores. Data moves between devices by JAX's collectives and lax.ppermute only.
A program may use at most 128 MiB of HBM per device.

v0:
```python
import functools

import jax
import jax.numpy as jnp
from jax import lax
from jax.experimental import pallas as pl
from jax.experimental.pallas import tpu as pltpu
from jax.sharding import PartitionSpec as P


QUERY_HEADS = 40
KEY_VALUE_HEADS = 8
HEAD_SIZE = 128
NCAND = 128
PEER = 2
SAMPLES = 16
GROUP = QUERY_HEADS // KEY_VALUE_HEADS
LANES = 128
TEAM = 4
BIG_NEG = -1e30


VMEM = pltpu.VMEM
F32 = jnp.float32
BF16 = jnp.bfloat16


def params(mib=48):
    return pltpu.CompilerParams(vmem_limit_bytes=mib * 1024 * 1024)


def round16(count):
    return (count + 15) // 16 * 16


def note_rows(count):
    return round16(count)


def find_slots(tags_ref, slot_ref, count_ref, chains_here, owners):
    def clear(o, _):
        count_ref[o] = 0
        for k in range(PEER):
            slot_ref[o * PEER + k] = -1
        return 0

    lax.fori_loop(0, owners, clear, 0)

    def place(s, _):
        owner = tags_ref[s] // chains_here
        rank = jnp.minimum(count_ref[owner], PEER - 1)
        slot_ref[owner * PEER + rank] = s
        count_ref[owner] = rank + 1
        return 0

    lax.fori_loop(0, tags_ref.shape[0], place, 0)


def pack_kernel(jobs, chains_here, owners, tags_hbm, cache_ref, *refs):
    outs = refs[: len(jobs)]
    tags_ref, slot_ref, count_ref, tag_sem, sem = refs[len(jobs) :]
    width = cache_ref.shape[2]
    fetch = pltpu.make_async_copy(tags_hbm, tags_ref, tag_sem)
    fetch.start()
    position = lax.axis_index("dp")
    row, high, high_count = lax.rem(position, TEAM), position // TEAM, owners // TEAM
    fetch.wait()
    find_slots(tags_ref, slot_ref, count_ref, chains_here, owners)
    copies = []
    for out, (offset, first, classes) in zip(outs, jobs):
        member = row ^ offset
        blocks = classes * PEER
        note = jnp.full((note_rows(blocks), out.shape[1]), float(chains_here), F32)
        line = lax.broadcasted_iota(jnp.int32, note.shape, 0)
        for h in range(classes):
            owner = lax.rem(high + first + h, high_count) * TEAM + member
            for k in range(PEER):
                slot = slot_ref[owner * PEER + k]
                safe = jnp.maximum(slot, 0)
                chain = jnp.where(slot < 0, chains_here, tags_ref[safe] % chains_here)
                index = h * PEER + k
                for part in range(2):
                    copy = pltpu.make_async_copy(
                        cache_ref.at[safe, part],
                        out.at[pl.ds((index * 2 + part) * width, width)],
                        sem.at[len(copies)],
                    )
                    copy.start()
                    copies.append(copy)
                note = jnp.where(line == index, chain.astype(F32), note)
        out[pl.ds(blocks * 2 * width, note_rows(blocks)), :] = note.astype(BF16)
    for copy in copies:
        copy.wait()


def pack(jobs, chains_here, owners, tags, cache):
    width, lanes = cache.shape[2], cache.shape[3]
    shapes = []
    for _, _, classes in jobs:
        blocks = classes * PEER
        shapes.append(jax.ShapeDtypeStruct((blocks * 2 * width + note_rows(blocks), lanes), BF16))
    moved = sum(s.shape[0] * s.shape[1] * 2 for s in shapes)
    count = sum(classes * PEER * 2 for _, _, classes in jobs)
    return pl.pallas_call(
        functools.partial(pack_kernel, jobs, chains_here, owners),
        out_shape=tuple(shapes),
        in_specs=[pl.BlockSpec(memory_space=pltpu.HBM)] * 2,
        out_specs=tuple(pl.BlockSpec(memory_space=VMEM) for _ in jobs),
        scratch_shapes=[
            pltpu.SMEM(tags.shape, jnp.int32),
            pltpu.SMEM((owners * PEER,), jnp.int32),
            pltpu.SMEM((owners,), jnp.int32),
            pltpu.SemaphoreType.DMA,
            pltpu.SemaphoreType.DMA((count,)),
        ],
        compiler_params=params(51),
        cost_estimate=pl.CostEstimate(flops=0, bytes_accessed=2 * moved, transcendentals=0),
    )(tags, cache)


def query_rows(q_ref, lead, g):
    chains = q_ref.shape[-3]
    tiles = []
    for c in range(chains):
        for j in range(GROUP):
            at = (g * GROUP + j) * HEAD_SIZE
            tiles.append(q_ref[lead + (c, slice(None), pl.ds(at, HEAD_SIZE))])
    return jnp.concatenate(tiles, axis=0)


def dot_nt(a, b):
    return lax.dot_general(a, b, (((1,), (1,)), ((), ())), preferred_element_type=F32)


def block_tiles(sources, h, classes, g, queries, chain_of_row, width):
    scale = HEAD_SIZE**-0.5
    tiles = []
    for source in sources:
        notes = source[pl.ds(classes * PEER * 2 * width, note_rows(classes * PEER)), pl.ds(0, width)].astype(F32)
        for k in range(PEER):
            index = h * PEER + k
            keys = source[pl.ds(index * 2 * width, width), pl.ds(g * HEAD_SIZE, HEAD_SIZE)]
            values = source[pl.ds((index * 2 + 1) * width, width), pl.ds(g * HEAD_SIZE, HEAD_SIZE)]
            valid = notes[index : index + 1, :] == chain_of_row
            scores = jnp.where(valid, dot_nt(queries, keys) * scale, BIG_NEG)
            tiles.append((scores, valid, values))
    return tiles


def reduce_tiles(tiles):
    peak = functools.reduce(jnp.maximum, [jnp.max(s, axis=1, keepdims=True) for s, _, _ in tiles])
    total, summed = None, None
    for scores, valid, values in tiles:
        weights = jnp.where(valid, jnp.exp(scores - peak), 0.0)
        part = jnp.sum(weights, axis=1, keepdims=True)
        added = jnp.dot(weights.astype(BF16), values, preferred_element_type=F32)
        total = part if total is None else total + part
        summed = added if summed is None else summed + added
    return peak, total, summed


def diagonal(rows):
    return lax.broadcasted_iota(jnp.int32, (rows, LANES), 0) == lax.broadcasted_iota(jnp.int32, (rows, LANES), 1)


def pieces_of(rows):
    return [(at, min(LANES, rows - at)) for at in range(0, rows, LANES)]


def fold_kernel(classes, width, *refs):
    q_refs, sources, out_refs = refs[:classes], refs[classes : classes + TEAM], refs[classes + TEAM :]
    chains, span = q_refs[0].shape[0], q_refs[0].shape[1]
    rows = chains * GROUP * span
    heads = q_refs[0].shape[2] // HEAD_SIZE // GROUP
    chain_of_row = (lax.broadcasted_iota(jnp.int32, (rows, width), 0) // (GROUP * span)).astype(F32)
    cuts = pieces_of(rows)
    for h in range(classes):
        out_ref = out_refs[h]
        line = lax.broadcasted_iota(jnp.int32, (out_ref.shape[0] - heads * rows, LANES), 0)
        tail = jnp.zeros(line.shape, F32)
        for g in range(heads):
            queries = query_rows(q_refs[h], (), g)
            peak, total, summed = reduce_tiles(
                block_tiles(sources, h, classes, g, queries, chain_of_row, width)
            )
            empty = total <= 0.0
            safe = jnp.where(empty, 1.0, total)
            out_ref[pl.ds(g * rows, rows), :] = (summed / safe).astype(BF16)
            logs = jnp.where(empty, BIG_NEG, peak + jnp.log(safe))
            for i, (at, size) in enumerate(cuts):
                flat = jnp.sum(
                    jnp.where(diagonal(size), logs[at : at + size, :], 0.0), axis=0, keepdims=True
                )
                first = flat.astype(BF16).astype(F32)
                rest = flat - first
                second = rest.astype(BF16).astype(F32)
                third = rest - second
                for p, piece in enumerate((first, second, third)):
                    at_line = (p * heads + g) * len(cuts) + i
                    tail = jnp.where(line == at_line, piece, tail)
        out_ref[pl.ds(heads * rows, line.shape[0]), :] = tail.astype(BF16)


def message_rows(rows, heads):
    return heads * rows + round16(3 * heads * len(pieces_of(rows)))


def fold(queries, sources, width):
    classes = len(queries)
    chains, span, features = queries[0].shape
    rows, heads = chains * GROUP * span, features // HEAD_SIZE // GROUP
    flops = 4 * classes * heads * rows * TEAM * PEER * width * HEAD_SIZE
    return pl.pallas_call(
        functools.partial(fold_kernel, classes, width),
        out_shape=tuple(
            jax.ShapeDtypeStruct((message_rows(rows, heads), LANES), BF16) for _ in range(classes)
        ),
        in_specs=[pl.BlockSpec(memory_space=VMEM)] * (classes + TEAM),
        out_specs=tuple(pl.BlockSpec(memory_space=VMEM) for _ in range(classes)),
        compiler_params=params(),
        cost_estimate=pl.CostEstimate(flops=flops, bytes_accessed=1 << 20, transcendentals=0),
    )(*queries, *sources)


def finish_kernel(classes, width, *refs):
    q_ref, span_ref, w_ref = refs[:3]
    sources = refs[3 : 3 + TEAM]
    partials = refs[3 + TEAM : 3 + TEAM + classes]
    attended_ref, logits_ref = refs[3 + TEAM + classes :]
    chains, span = q_ref.shape[0], q_ref.shape[1]
    rows = chains * GROUP * span
    heads = q_ref.shape[2] // HEAD_SIZE // GROUP
    scale = HEAD_SIZE**-0.5
    chain_of_row = (lax.broadcasted_iota(jnp.int32, (rows, width), 0) // (GROUP * span)).astype(F32)
    shape = (rows, chains * span)
    row, key = lax.broadcasted_iota(jnp.int32, shape, 0), lax.broadcasted_iota(jnp.int32, shape, 1)
    causal = (row // (GROUP * span) == key // span) & (row % span >= key % span)
    cuts = pieces_of(rows)
    logits = jnp.zeros(logits_ref.shape, F32)
    for g in range(heads):
        queries = query_rows(q_ref, (), g)
        tiles = block_tiles(sources, 0, 1, g, queries, chain_of_row, width)
        lanes = pl.ds(g * HEAD_SIZE, HEAD_SIZE)
        keys = jnp.concatenate([span_ref[c, 0, :, lanes] for c in range(chains)], axis=0)
        values = jnp.concatenate([span_ref[c, 1, :, lanes] for c in range(chains)], axis=0)
        scores = jnp.where(causal, dot_nt(queries, keys) * scale, BIG_NEG)
        tiles.append((scores, causal, values))
        peak, total, summed = reduce_tiles(tiles)
        for partial in partials:
            tail = partial[pl.ds(heads * rows, partial.shape[0] - heads * rows), :].astype(F32)
            columns = []
            for i, (at, size) in enumerate(cuts):
                lines = [(p * heads + g) * len(cuts) + i for p in range(3)]
                flat = sum(tail[n : n + 1, :] for n in lines)
                columns.append(jnp.sum(jnp.where(diagonal(size), flat, 0.0), axis=1, keepdims=True))
            logs = jnp.concatenate(columns, axis=0)
            best = jnp.maximum(peak, logs)
            left, right = jnp.exp(peak - best), jnp.exp(logs - best)
            other = partial[pl.ds(g * rows, rows), :].astype(F32)
            summed = summed * left + other * right
            total = total * left + right
            peak = best
        result = (summed / total).astype(BF16)
        for j in range(GROUP):
            at = (g * GROUP + j) * HEAD_SIZE
            picked = []
            for c in range(chains):
                part = result[(c * GROUP + j) * span : (c * GROUP + j + 1) * span, :]
                attended_ref[c, :, pl.ds(at, HEAD_SIZE)] = part
                picked.append(part)
            logits = logits + jnp.dot(
                jnp.concatenate(picked, axis=0),
                w_ref[pl.ds(at, HEAD_SIZE), :],
                preferred_element_type=F32,
            )
    logits_ref[...] = logits


def finish(queries, span_key_value, w_cand, sources, partials, width):
    chains, span, _ = queries.shape
    return pl.pallas_call(
        functools.partial(finish_kernel, len(partials), width),
        out_shape=(
            jax.ShapeDtypeStruct(queries.shape, BF16),
            jax.ShapeDtypeStruct((chains * span, NCAND), F32),
        ),
        in_specs=[pl.BlockSpec(memory_space=VMEM)] * (3 + TEAM + len(partials)),
        out_specs=(pl.BlockSpec(memory_space=VMEM),) * 2,
        compiler_params=params(),
        cost_estimate=pl.CostEstimate(flops=1 << 27, bytes_accessed=1 << 20, transcendentals=0),
    )(queries, span_key_value, w_cand, *sources, *partials)


def score_kernel(answer_ref, gathered_ref, score_ref, tally_ref):
    parts = gathered_ref.shape[0]
    position = lax.axis_index("dp")
    chains = score_ref.shape[0]
    span = gathered_ref.shape[1] // chains
    logits = functools.reduce(lambda a, b: a + b, [gathered_ref[p] for p in range(parts)])
    top = jnp.max(logits, axis=1, keepdims=True)
    norm = top + jnp.log(jnp.sum(jnp.exp(logits - top), axis=1, keepdims=True))
    lane = lax.broadcasted_iota(jnp.int32, (span, NCAND), 1)
    line = lax.broadcasted_iota(jnp.int32, tally_ref.shape, 0)
    column = lax.broadcasted_iota(jnp.int32, tally_ref.shape, 1)
    tally = jnp.zeros(tally_ref.shape, F32)
    for c in range(chains):
        here = slice(c * span, (c + 1) * span)
        chosen = jnp.sum(jnp.where(lane == answer_ref[c], logits[here], 0.0), axis=1, keepdims=True)
        score = jnp.sum(chosen - norm[here], axis=0, keepdims=True) / span
        score_ref[c : c + 1, :] = jnp.broadcast_to(score, (1, NCAND))
        prompt = (position * chains + c) // SAMPLES
        tally = tally + jnp.where((line == prompt) & (column == answer_ref[c]), score, 0.0)
    tally_ref[...] = tally


def score(gathered, answer_id, prompts):
    chains = answer_id.shape[0]
    return pl.pallas_call(
        score_kernel,
        out_shape=(
            jax.ShapeDtypeStruct((chains, NCAND), F32),
            jax.ShapeDtypeStruct((prompts, NCAND), F32),
        ),
        in_specs=[pl.BlockSpec(memory_space=pltpu.SMEM), pl.BlockSpec(memory_space=VMEM)],
        out_specs=(pl.BlockSpec(memory_space=VMEM),) * 2,
        compiler_params=params(8),
        cost_estimate=pl.CostEstimate(flops=1 << 20, bytes_accessed=1 << 16, transcendentals=0),
    )(answer_id, gathered)


def program(queries, key_value_cache, slot_tags, span_key_value, answer_id, w_cand):
    owners = lax.axis_size("dp")
    chains_here = queries.shape[0]
    width = key_value_cache.shape[2]
    teams = owners // TEAM
    others = teams - 1

    def across(array, step):
        pairs = [(((t + step) % teams) * TEAM + r, t * TEAM + r) for t in range(teams) for r in range(TEAM)]
        return lax.ppermute(array, "dp", pairs)

    def within(array, offset):
        return lax.ppermute(array, "dp", [(i, i ^ offset) for i in range(owners)])

    offsets = range(1, TEAM)
    jobs = [(j, 1, others) for j in offsets] + [(j, 0, 1) for j in offsets] + [(0, 1, others), (0, 0, 1)]
    messages = pack(jobs, chains_here, owners, slot_tags, key_value_cache)
    far_in = [within(m, j) for m, j in zip(messages, offsets)]
    visiting = [across(queries, step) for step in range(1, teams)]
    near_in = [within(m, j) for m, j in zip(messages[TEAM - 1 :], offsets)]
    own_far, own_near = messages[-2:]
    folded = fold(visiting, [own_far] + far_in, width)
    partials = [across(m, teams - step) for m, step in zip(folded, range(1, teams))]
    attended, partial_logits = finish(
        queries, span_key_value, w_cand, [own_near] + near_in, partials, width
    )
    gathered = lax.all_gather(partial_logits, "mp")
    prompts = owners * chains_here // SAMPLES
    scores, tally = score(gathered, answer_id, prompts)
    chain_score = scores[:, 0]
    step = 1
    while step < owners:
        tally = tally + within(tally, step)
        step *= 2
    per = NCAND // owners
    answer_tally = lax.dynamic_slice_in_dim(tally, lax.axis_index("dp") * per, per, axis=1)
    return attended, chain_score, answer_tally


def solution(mesh):
    in_specs = (
        P("dp", None, "mp"),
        P("dp", None, None, "mp"),
        P("dp"),
        P("dp", None, None, "mp"),
        P("dp"),
        P("mp", None),
    )
    out_specs = (P("dp", None, "mp"), P("dp"), P(None, "dp"))
    return jax.shard_map(program, mesh=mesh, in_specs=in_specs, out_specs=out_specs, check_vma=False)
```

profile of v0, /device:TPU:0, one launch (start us, length us, event | category | flops | bytes accessed | tf_op | source)
XLA Modules:
  0.0 59.0 jit_solution(14656202639629504228)
XLA Ops:
  0.6 0.0 copy-start.1
  0.6 0.0 copy-start
  0.7 0.0 copy-start.2
  0.7 0.0 copy-start.3
  0.7 0.7 %copy-done.3 = s32[16]{0:T(128)S(1)} copy-done((s32[16]{0:T(128)S(1)}, s32[16]{0:T(128)}, u32[]{:S(2)}) %copy-start.3) | copy-done | bytes 88
  1.4 0.0 copy-start.4
  1.4 2.8 %shard_map.85 = (bf16[528,256]{1,0:T(8,128)(2,1)S(1)}, bf16[528,256]{1,0:T(8,128)(2,1)S(1)}, bf16[528,256]{1,0:T(8,128)(2,1)S(1)}, bf16[528,256]{1,0:T(8,128)(2,...) custom-call(s32[16]{0:T(128)S(1)} %copy-done.3, ...), custom_call_target="tpu_custom_call" | custom-call | bytes 4325376 | tf_op jit(solution)/shard_map/pallas_call | solution.py:104
  4.2 3.0 %collective-permute-start.4 = (bf16[528,256]{1,0:T(8,128)(2,1)S(1)}, bf16[528,256]{1,0:T(8,128)(2,1)S(1)}, u32[]{:S(2)}, u32[]{:S(2)}) collective-permute-start(bf16[528,256]{1,0:T(8,128)(2,1)S(1)} %get-tuple-element.20), channel_id=1, source_target_pairs={{0,4},{4,0},{8,12},{12,8},{16,20},{20,16},{24,28},{28,24},{1,5},{5... | collective-permute-start | bytes 811016 | tf_op jit(solution)/shard_map/ppermute | solution.py:343
  7.2 1.6 %collective-permute-start.5 = (bf16[528,256]{1,0:T(8,128)(2,1)S(1)}, bf16[528,256]{1,0:T(8,128)(2,1)S(1)}, u32[]{:S(2)}, u32[]{:S(2)}) collective-permute-start(bf16[528,256]{1,0:T(8,128)(2,1)S(1)} %get-tuple-element.21), channel_id=1, source_target_pairs={{0,8},{4,12},{8,0},{12,4},{16,24},{20,28},{24,16},{28,20},{1,9},{5... | collective-permute-start | bytes 811016 | tf_op jit(solution)/shard_map/ppermute | solution.py:343
  8.8 0.0 collective-permute-start.6
  8.8 0.0 copy-done.1
  8.8 3.0 %collective-permute-start.3 = (bf16[2,16,1280]{2,1,0:T(8,128)(2,1)S(1)}, bf16[2,16,1280]{2,1,0:T(8,128)(2,1)S(1)}, u32[]{:S(2)}, u32[]{:S(2)}) collective-permute-start(bf16[2,16,1280]{2,1,0:T(8,128)(2,1)S(1)} %copy-done.1), channel_id=1, source_target_pairs={{16,0},{20,4},{24,8},{28,12},{0,16},{4,20},{8,24},{12,28},{17,1},{... | collective-permute-start | bytes 245768 | tf_op jit(solution)/shard_map/ppermute | solution.py:340
  11.8 1.5 %collective-permute-start = (bf16[528,256]{1,0:T(8,128)(2,1)S(1)}, bf16[528,256]{1,0:T(8,128)(2,1)S(1)}, u32[]{:S(2)}, u32[]{:S(2)}) collective-permute-start(bf16[528,256]{1,0:T(8,128)(2,1)S(1)} %get-tuple-element.16), channel_id=1, source_target_pairs={{0,4},{4,0},{8,12},{12,8},{16,20},{20,16},{24,28},{28,24},{1,5},{5... | collective-permute-start | bytes 811016 | tf_op jit(solution)/shard_map/ppermute | solution.py:343
  13.3 8.5 %collective-permute-done.3.refs_0_ = bf16[2,16,1280]{2,1,0:T(8,128)(2,1)S(1)} collective-permute-done((bf16[2,16,1280]{2,1,0:T(8,128)(2,1)S(1)}, bf16[2,16,1280]{2,1,0:T(8,128)(2,1)S(1)}, u32[]{:S(2)}, u32[]{:S(2)}) %collective-permute-start.3) | collective-permute-done | bytes 81952 | tf_op jit(solution)/shard_map/ppermute | solution.py:340
  21.8 3.5 %collective-permute-start.1 = (bf16[528,256]{1,0:T(8,128)(2,1)S(1)}, bf16[528,256]{1,0:T(8,128)(2,1)S(1)}, u32[]{:S(2)}, u32[]{:S(2)}) collective-permute-start(bf16[528,256]{1,0:T(8,128)(2,1)S(1)} %get-tuple-element.17), channel_id=1, source_target_pairs={{0,8},{4,12},{8,0},{12,4},{16,24},{20,28},{24,16},{28,20},{1,9},{5... | collective-permute-start | bytes 811016 | tf_op jit(solution)/shard_map/ppermute | solution.py:343
  25.3 0.0 collective-permute-done.4.refs_2_
  25.3 0.0 collective-permute-start.2
  25.3 0.0 collective-permute-done.5.refs_3_
  25.3 0.0 collective-permute-done.6.refs_4_
  25.3 1.2 %shard_map.86 = bf16[336,128]{1,0:T(8,128)(2,1)S(1)} custom-call(bf16[2,16,1280]{2,1,0:T(8,128)(2,1)S(1)} %collective-permute-done.3.refs_0_, bf16[528,256]{1,0:T(8,128)(2,1)S(1)} %get-tuple-element.19.refs_1_, bf16[528,256]{1,0:T(8,128)(2,1)S(1)} %collective-permute-done.4.refs_2_, bf16[528,256]{1,0:T(8,128)(2,1)S(1)} %collective-permute-done.5.refs_3_, ...), custom_call_target="tpu_custom_call" | custom-call | flops 167772160 | bytes 1048576 | tf_op jit(solution)/shard_map/pallas_call | solution.py:213
  26.6 1.9 %collective-permute-start.7 = (bf16[336,128]{1,0:T(8,128)(2,1)S(1)}, bf16[336,128]{1,0:T(8,128)(2,1)S(1)}, u32[]{:S(2)}, u32[]{:S(2)}) collective-permute-start(bf16[336,128]{1,0:T(8,128)(2,1)S(1)} %shard_map.86), channel_id=1, source_target_pairs={{16,0},{20,4},{24,8},{28,12},{0,16},{4,20},{8,24},{12,28},{17,1},{... | collective-permute-start | bytes 258056 | tf_op jit(solution)/shard_map/ppermute | solution.py:340
  28.5 0.0 collective-permute-done.refs_4_
  28.5 6.0 %collective-permute-done.1.refs_5_ = bf16[528,256]{1,0:T(8,128)(2,1)S(1)} collective-permute-done((bf16[528,256]{1,0:T(8,128)(2,1)S(1)}, bf16[528,256]{1,0:T(8,128)(2,1)S(1)}, u32[]{:S(2)}, u32[]{:S(2)}) %collective-permute-start.1) | collective-permute-done | bytes 270368 | tf_op jit(solution)/shard_map/ppermute | solution.py:343
  34.5 3.8 %collective-permute-done.2.refs_6_ = bf16[528,256]{1,0:T(8,128)(2,1)S(1)} collective-permute-done((bf16[528,256]{1,0:T(8,128)(2,1)S(1)}, bf16[528,256]{1,0:T(8,128)(2,1)S(1)}, u32[]{:S(2)}, u32[]{:S(2)}) %collective-permute-start.2) | collective-permute-done | bytes 270368 | tf_op jit(solution)/shard_map/ppermute | solution.py:343
  38.3 0.0 collective-permute-done.7.refs_7_
  38.3 0.0 copy-done
  38.3 0.0 copy-done.2
  38.3 2.5 %shard_map.87 = (bf16[2,16,1280]{2,1,0:T(8,128)(2,1)}, f32[32,128]{1,0:T(8,128)S(1)}) custom-call(bf16[2,16,1280]{2,1,0:T(8,128)(2,1)S(1)} %copy-done.1, bf16[2,2,16,256]{3,2,1,0:T(8,128)(2,1)S(1)} %copy-done.2, bf16[1280,128]{1,0:T(8,128)(2,1)S(1)} %copy-done, bf16[528,256]{1,0:T(8,128)(2,1)S(1)} %get-tuple-element.15.refs_3_, ...), custom_call_target="tpu_custom_call" | custom-call | flops 134217728 | bytes 1048576 | tf_op jit(solution)/shard_map/pallas_call | solution.py:281
  40.8 5.2 %all-gather = f32[128,128]{1,0:T(8,128)S(1)} all-gather(f32[32,128]{1,0:T(8,128)S(1)} %get-tuple-element.24), channel_id=2, replica_groups=mesh['dp'=8,'mp'=4] {'mp'}, dimensions={0}, use_global_device_ids=true | all-gather | bytes 81920 | tf_op jit(solution)/shard_map/all_gather | solution.py:357
  46.1 0.0 copy-done.4
  46.1 0.7 %shard_map.88 = (f32[2,128]{1,0:T(2,128)S(1)}, f32[1,128]{1,0:T(1,128)S(1)}) custom-call(s32[2]{0:T(128)S(1)} %copy-done.4, f32[4,32,128]{2,1,0:T(8,128)S(1)} %bitcast.1), custom_call_target="tpu_custom_call" | custom-call | flops 1048576 | bytes 65536 | tf_op jit(solution)/shard_map/pallas_call | solution.py:318
  46.8 1.3 %collective-permute-start.8 = (f32[1,128]{1,0:T(1,128)S(1)}, f32[1,128]{1,0:T(1,128)S(1)}, u32[]{:S(2)}, u32[]{:S(2)}) collective-permute-start(f32[1,128]{1,0:T(1,128)S(1)} %get-tuple-element.26), channel_id=1, source_target_pairs={{0,4},{4,0},{8,12},{12,8},{16,20},{20,16},{24,28},{28,24},{1,5},{5... | collective-permute-start | bytes 1544 | tf_op jit(solution)/shard_map/ppermute | solution.py:343
  48.0 2.4 %collective-permute-done.8 = f32[1,128]{1,0:T(1,128)S(1)} collective-permute-done((f32[1,128]{1,0:T(1,128)S(1)}, f32[1,128]{1,0:T(1,128)S(1)}, u32[]{:S(2)}, u32[]{:S(2)}) %collective-permute-start.8) | collective-permute-done | bytes 544 | tf_op jit(solution)/shard_map/ppermute | solution.py:343
  50.4 1.7 %collective-permute-start.9 = (f32[1,128]{1,0:T(1,128)S(1)}, f32[1,128]{1,0:T(1,128)S(1)}, u32[]{:S(2)}, u32[]{:S(2)}) collective-permute-start(f32[1,128]{1,0:T(1,128)S(1)} %add.12), channel_id=1, source_target_pairs={{0,8},{4,12},{8,0},{12,4},{16,24},{20,28},{24,16},{28,20},{1,9},{5... | collective-permute-start | bytes 1544 | tf_op jit(solution)/shard_map/ppermute | solution.py:343
  52.1 1.9 %collective-permute-done.9 = f32[1,128]{1,0:T(1,128)S(1)} collective-permute-done((f32[1,128]{1,0:T(1,128)S(1)}, f32[1,128]{1,0:T(1,128)S(1)}, u32[]{:S(2)}, u32[]{:S(2)}) %collective-permute-start.9) | collective-permute-done | bytes 544 | tf_op jit(solution)/shard_map/ppermute | solution.py:343
  54.0 2.4 %collective-permute-start.10 = (f32[1,128]{1,0:T(1,128)S(1)}, f32[1,128]{1,0:T(1,128)S(1)}, u32[]{:S(2)}, u32[]{:S(2)}) collective-permute-start(f32[1,128]{1,0:T(1,128)S(1)} %add.13), channel_id=1, source_target_pairs={{0,16},{4,20},{8,24},{12,28},{16,0},{20,4},{24,8},{28,12},{1,17},{... | collective-permute-start | bytes 1544 | tf_op jit(solution)/shard_map/ppermute | solution.py:343
  56.4 0.6 %slice_reduce_fusion = f32[2]{0:T(128)} fusion(f32[2,128]{1,0:T(2,128)S(1)} %get-tuple-element.25), kind=kLoop, calls=%fused_computation | loop fusion | bytes 16 | tf_op jit(solution)/shard_map/slice | solution.py:360
  57.0 1.5 %collective-permute-done.10 = f32[1,128]{1,0:T(1,128)S(1)} collective-permute-done((f32[1,128]{1,0:T(1,128)S(1)}, f32[1,128]{1,0:T(1,128)S(1)}, u32[]{:S(2)}, u32[]{:S(2)}) %collective-permute-start.10) | collective-permute-done | bytes 544 | tf_op jit(solution)/shard_map/ppermute | solution.py:343
  58.5 0.6 constant_dynamic-slice_fusion
  (3 shorter events, 0.0 us)
Async XLA Ops:
  0.6 8.1 %copy-start.1 = (bf16[2,16,1280]{2,1,0:T(8,128)(2,1)S(1)}, bf16[2,16,1280]{2,1,0:T(8,128)(2,1)}, u32[]{:S(2)}) copy-start(bf16[2,16,1280]{2,1,0:T(8,128)(2,1)} %refs_0_.1) | copy-start | bytes 245764
  0.6 37.6 %copy-start = (bf16[1280,128]{1,0:T(8,128)(2,1)S(1)}, bf16[1280,128]{1,0:T(8,128)(2,1)}, u32[]{:S(2)}) copy-start(bf16[1280,128]{1,0:T(8,128)(2,1)} %refs_2_.1) | copy-start | bytes 983044
  0.7 37.6 %copy-start.2 = (bf16[2,2,16,256]{3,2,1,0:T(8,128)(2,1)S(1)}, bf16[2,2,16,256]{3,2,1,0:T(8,128)(2,1)}, u32[]{:S(2)}) copy-start(bf16[2,2,16,256]{3,2,1,0:T(8,128)(2,1)} %refs_1_.1) | copy-start | bytes 98308
  0.7 0.7 %copy-start.3 = (s32[16]{0:T(128)S(1)}, s32[16]{0:T(128)}, u32[]{:S(2)}) copy-start(s32[16]{0:T(128)} %tags_hbm.1) | copy-start | bytes 196
  1.4 44.7 %copy-start.4 = (s32[2]{0:T(128)S(1)}, s32[2]{0:T(128)}, u32[]{:S(2)}) copy-start(s32[2]{0:T(128)} %answer_ref.1) | copy-start | bytes 28
  4.2 21.2 %collective-permute-start.4 = (bf16[528,256]{1,0:T(8,128)(2,1)S(1)}, bf16[528,256]{1,0:T(8,128)(2,1)S(1)}, u32[]{:S(2)}, u32[]{:S(2)}) collective-permute-start(bf16[528,256]{1,0:T(8,128)(2,1)S(1)} %get-tuple-element.20), channel_id=1, source_target_pairs={{0,4},{4,0},{8,12},{12,8},{16,20},{20,16},{24,28},{28,24},{1,5},{5... | collective-permute-start | bytes 811016 | tf_op jit(solution)/shard_map/ppermute | solution.py:343
  7.2 18.1 %collective-permute-start.5 = (bf16[528,256]{1,0:T(8,128)(2,1)S(1)}, bf16[528,256]{1,0:T(8,128)(2,1)S(1)}, u32[]{:S(2)}, u32[]{:S(2)}) collective-permute-start(bf16[528,256]{1,0:T(8,128)(2,1)S(1)} %get-tuple-element.21), channel_id=1, source_target_pairs={{0,8},{4,12},{8,0},{12,4},{16,24},{20,28},{24,16},{28,20},{1,9},{5... | collective-permute-start | bytes 811016 | tf_op jit(solution)/shard_map/ppermute | solution.py:343
  8.8 16.6 %collective-permute-start.6 = (bf16[528,256]{1,0:T(8,128)(2,1)S(1)}, bf16[528,256]{1,0:T(8,128)(2,1)S(1)}, u32[]{:S(2)}, u32[]{:S(2)}) collective-permute-start(bf16[528,256]{1,0:T(8,128)(2,1)S(1)} %get-tuple-element.22), channel_id=1, source_target_pairs={{0,12},{4,8},{8,4},{12,0},{16,28},{20,24},{24,20},{28,16},{1,13},{... | collective-permute-start | bytes 811016 | tf_op jit(solution)/shard_map/ppermute | solution.py:343
  8.8 13.0 %collective-permute-start.3 = (bf16[2,16,1280]{2,1,0:T(8,128)(2,1)S(1)}, bf16[2,16,1280]{2,1,0:T(8,128)(2,1)S(1)}, u32[]{:S(2)}, u32[]{:S(2)}) collective-permute-start(bf16[2,16,1280]{2,1,0:T(8,128)(2,1)S(1)} %copy-done.1), channel_id=1, source_target_pairs={{16,0},{20,4},{24,8},{28,12},{0,16},{4,20},{8,24},{12,28},{17,1},{... | collective-permute-start | bytes 245768 | tf_op jit(solution)/shard_map/ppermute | solution.py:340
  11.8 16.7 %collective-permute-start = (bf16[528,256]{1,0:T(8,128)(2,1)S(1)}, bf16[528,256]{1,0:T(8,128)(2,1)S(1)}, u32[]{:S(2)}, u32[]{:S(2)}) collective-permute-start(bf16[528,256]{1,0:T(8,128)(2,1)S(1)} %get-tuple-element.16), channel_id=1, source_target_pairs={{0,4},{4,0},{8,12},{12,8},{16,20},{20,16},{24,28},{28,24},{1,5},{5... | collective-permute-start | bytes 811016 | tf_op jit(solution)/shard_map/ppermute | solution.py:343
  21.8 12.7 %collective-permute-start.1 = (bf16[528,256]{1,0:T(8,128)(2,1)S(1)}, bf16[528,256]{1,0:T(8,128)(2,1)S(1)}, u32[]{:S(2)}, u32[]{:S(2)}) collective-permute-start(bf16[528,256]{1,0:T(8,128)(2,1)S(1)} %get-tuple-element.17), channel_id=1, source_target_pairs={{0,8},{4,12},{8,0},{12,4},{16,24},{20,28},{24,16},{28,20},{1,9},{5... | collective-permute-start | bytes 811016 | tf_op jit(solution)/shard_map/ppermute | solution.py:343
  25.3 12.9 %collective-permute-start.2 = (bf16[528,256]{1,0:T(8,128)(2,1)S(1)}, bf16[528,256]{1,0:T(8,128)(2,1)S(1)}, u32[]{:S(2)}, u32[]{:S(2)}) collective-permute-start(bf16[528,256]{1,0:T(8,128)(2,1)S(1)} %get-tuple-element.18), channel_id=1, source_target_pairs={{0,12},{4,8},{8,4},{12,0},{16,28},{20,24},{24,20},{28,16},{1,13},{... | collective-permute-start | bytes 811016 | tf_op jit(solution)/shard_map/ppermute | solution.py:343
  26.6 11.7 %collective-permute-start.7 = (bf16[336,128]{1,0:T(8,128)(2,1)S(1)}, bf16[336,128]{1,0:T(8,128)(2,1)S(1)}, u32[]{:S(2)}, u32[]{:S(2)}) collective-permute-start(bf16[336,128]{1,0:T(8,128)(2,1)S(1)} %shard_map.86), channel_id=1, source_target_pairs={{16,0},{20,4},{24,8},{28,12},{0,16},{4,20},{8,24},{12,28},{17,1},{... | collective-permute-start | bytes 258056 | tf_op jit(solution)/shard_map/ppermute | solution.py:340
  46.8 3.6 %collective-permute-start.8 = (f32[1,128]{1,0:T(1,128)S(1)}, f32[1,128]{1,0:T(1,128)S(1)}, u32[]{:S(2)}, u32[]{:S(2)}) collective-permute-start(f32[1,128]{1,0:T(1,128)S(1)} %get-tuple-element.26), channel_id=1, source_target_pairs={{0,4},{4,0},{8,12},{12,8},{16,20},{20,16},{24,28},{28,24},{1,5},{5... | collective-permute-start | bytes 1544 | tf_op jit(solution)/shard_map/ppermute | solution.py:343
  50.4 3.6 %collective-permute-start.9 = (f32[1,128]{1,0:T(1,128)S(1)}, f32[1,128]{1,0:T(1,128)S(1)}, u32[]{:S(2)}, u32[]{:S(2)}) collective-permute-start(f32[1,128]{1,0:T(1,128)S(1)} %add.12), channel_id=1, source_target_pairs={{0,8},{4,12},{8,0},{12,4},{16,24},{20,28},{24,16},{28,20},{1,9},{5... | collective-permute-start | bytes 1544 | tf_op jit(solution)/shard_map/ppermute | solution.py:343
  54.0 4.5 %collective-permute-start.10 = (f32[1,128]{1,0:T(1,128)S(1)}, f32[1,128]{1,0:T(1,128)S(1)}, u32[]{:S(2)}, u32[]{:S(2)}) collective-permute-start(f32[1,128]{1,0:T(1,128)S(1)} %add.13), channel_id=1, source_target_pairs={{0,16},{4,20},{8,24},{12,28},{16,0},{20,4},{24,8},{28,12},{1,17},{... | collective-permute-start | bytes 1544 | tf_op jit(solution)/shard_map/ppermute | solution.py:343
where the time goes:
time: 59.3 us; the launch traced here: 59 us
  waiting for transfers between devices  24.1 us (41%)
  starting transfers between devices  19.8 us (33%)
  Pallas kernels  7.27 us (12%)
  blocking collectives  5.22 us (9%)
  local copies, waits for them, and re-layouts  1.92 us (3%)
  between operations  0.72 us (1%)
    ppermute x9, waiting for transfers between devices, within(): return lax.ppermute(array, 'dp', [(i, i ^ offset) for i in range(owners)])  15.5 us
    ppermute x9, starting transfers between devices, within(): return lax.ppermute(array, 'dp', [(i, i ^ offset) for i in range(owners)])  14.9 us
    ppermute x2, waiting for transfers between devices, across(): return lax.ppermute(array, 'dp', pairs)  8.55 us
    all_gather x1, blocking collectives, program(): gathered = lax.all_gather(partial_logits, 'mp')  5.22 us
    ppermute x2, starting transfers between devices, across(): return lax.ppermute(array, 'dp', pairs)  4.94 us
    pallas_call x1, Pallas kernels, pack(): pl.pallas_call(functools.partial(pack_kernel, jobs, chains_here, owners),...  2.79 us
    pallas_call x1, Pallas kernels, finish(): pl.pallas_call(functools.partial(finish_kernel, len(partials), width), ou...  2.54 us
    pallas_call x1, Pallas kernels, fold(): pl.pallas_call(functools.partial(fold_kernel, classes, width), out_shape=...  1.22 us
  transfers between devices with their start and end apart: 11, of which 6 were waited for; matrix products, arithmetic and copies ran while one was open for 1% of the time, Pallas kernels for 2%

commit v1 on v0

--- a/solution.py
+++ b/solution.py
@@ -17,6 +17,7 @@
 GROUP = QUERY_HEADS // KEY_VALUE_HEADS
 LANES = 128
 TEAM = 4
+DIAGONAL = 3
 BIG_NEG = -1e30
 
 
@@ -34,7 +35,7 @@
 
 
 def note_rows(count):
-    return round16(count)
+    return (count + 7) // 8 * 8
 
 
 def find_slots(tags_ref, slot_ref, count_ref, chains_here, owners):
@@ -113,7 +114,7 @@
             pltpu.SemaphoreType.DMA,
             pltpu.SemaphoreType.DMA((count,)),
         ],
-        compiler_params=params(51),
+        compiler_params=params(),
         cost_estimate=pl.CostEstimate(flops=0, bytes_accessed=2 * moved, transcendentals=0),
     )(tags, cache)
 
@@ -167,8 +168,8 @@
     return [(at, min(LANES, rows - at)) for at in range(0, rows, LANES)]
 
 
-def fold_kernel(classes, width, *refs):
-    q_refs, sources, out_refs = refs[:classes], refs[classes : classes + TEAM], refs[classes + TEAM :]
+def fold_kernel(classes, held, width, *refs):
+    q_refs, sources, out_refs = refs[:classes], refs[classes : classes + held], refs[classes + held :]
     chains, span = q_refs[0].shape[0], q_refs[0].shape[1]
     rows = chains * GROUP * span
     heads = q_refs[0].shape[2] // HEAD_SIZE // GROUP
@@ -209,24 +210,23 @@
     classes = len(queries)
     chains, span, features = queries[0].shape
     rows, heads = chains * GROUP * span, features // HEAD_SIZE // GROUP
-    flops = 4 * classes * heads * rows * TEAM * PEER * width * HEAD_SIZE
+    held = len(sources)
+    flops = 4 * classes * heads * rows * held * PEER * width * HEAD_SIZE
     return pl.pallas_call(
-        functools.partial(fold_kernel, classes, width),
+        functools.partial(fold_kernel, classes, held, width),
         out_shape=tuple(
             jax.ShapeDtypeStruct((message_rows(rows, heads), LANES), BF16) for _ in range(classes)
         ),
-        in_specs=[pl.BlockSpec(memory_space=VMEM)] * (classes + TEAM),
+        in_specs=[pl.BlockSpec(memory_space=VMEM)] * (classes + held),
         out_specs=tuple(pl.BlockSpec(memory_space=VMEM) for _ in range(classes)),
         compiler_params=params(),
         cost_estimate=pl.CostEstimate(flops=flops, bytes_accessed=1 << 20, transcendentals=0),
     )(*queries, *sources)
 
 
-def finish_kernel(classes, width, *refs):
-    q_ref, span_ref, w_ref = refs[:3]
-    sources = refs[3 : 3 + TEAM]
-    partials = refs[3 + TEAM : 3 + TEAM + classes]
-    attended_ref, logits_ref = refs[3 + TEAM + classes :]
+def own_kernel(width, *refs):
+    q_ref, span_ref = refs[:2]
+    sources, (rows_ref, logs_ref) = refs[2:-2], refs[-2:]
     chains, span = q_ref.shape[0], q_ref.shape[1]
     rows = chains * GROUP * span
     heads = q_ref.shape[2] // HEAD_SIZE // GROUP
@@ -235,8 +235,6 @@
     shape = (rows, chains * span)
     row, key = lax.broadcasted_iota(jnp.int32, shape, 0), lax.broadcasted_iota(jnp.int32, shape, 1)
     causal = (row // (GROUP * span) == key // span) & (row % span >= key % span)
-    cuts = pieces_of(rows)
-    logits = jnp.zeros(logits_ref.shape, F32)
     for g in range(heads):
         queries = query_rows(q_ref, (), g)
         tiles = block_tiles(sources, 0, 1, g, queries, chain_of_row, width)
@@ -246,6 +244,34 @@
         scores = jnp.where(causal, dot_nt(queries, keys) * scale, BIG_NEG)
         tiles.append((scores, causal, values))
         peak, total, summed = reduce_tiles(tiles)
+        rows_ref[pl.ds(g * rows, rows), :] = summed / total
+        logs_ref[pl.ds(g * rows, rows), :] = jnp.broadcast_to(peak + jnp.log(total), (rows, LANES))
+
+
+def own(queries, span_key_value, sources, width):
+    chains, span, features = queries.shape
+    rows, heads = chains * GROUP * span, features // HEAD_SIZE // GROUP
+    flops = 4 * heads * rows * len(sources) * PEER * width * HEAD_SIZE
+    return pl.pallas_call(
+        functools.partial(own_kernel, width),
+        out_shape=(jax.ShapeDtypeStruct((heads * rows, LANES), F32),) * 2,
+        in_specs=[pl.BlockSpec(memory_space=VMEM)] * (2 + len(sources)),
+        out_specs=(pl.BlockSpec(memory_space=VMEM),) * 2,
+        compiler_params=params(),
+        cost_estimate=pl.CostEstimate(flops=flops, bytes_accessed=1 << 20, transcendentals=0),
+    )(queries, span_key_value, *sources)
+
+
+def finish_kernel(chains, span, *refs):
+    rows_ref, logs_ref, w_ref = refs[:3]
+    partials, (attended_ref, logits_ref) = refs[3:-2], refs[-2:]
+    rows = chains * GROUP * span
+    heads = rows_ref.shape[0] // rows
+    cuts = pieces_of(rows)
+    logits = jnp.zeros(logits_ref.shape, F32)
+    for g in range(heads):
+        here = pl.ds(g * rows, rows)
+        items = [(rows_ref[here, :], logs_ref[here, :])]
         for partial in partials:
             tail = partial[pl.ds(heads * rows, partial.shape[0] - heads * rows), :].astype(F32)
             columns = []
@@ -254,12 +280,11 @@
                 flat = sum(tail[n : n + 1, :] for n in lines)
                 columns.append(jnp.sum(jnp.where(diagonal(size), flat, 0.0), axis=1, keepdims=True))
             logs = jnp.concatenate(columns, axis=0)
-            best = jnp.maximum(peak, logs)
-            left, right = jnp.exp(peak - best), jnp.exp(logs - best)
-            other = partial[pl.ds(g * rows, rows), :].astype(F32)
-            summed = summed * left + other * right
-            total = total * left + right
-            peak = best
+            items.append((partial[here, :].astype(F32), logs))
+        best = functools.reduce(jnp.maximum, [logs for _, logs in items])
+        shares = [jnp.exp(logs - best) for _, logs in items]
+        total = functools.reduce(jnp.add, shares)
+        summed = functools.reduce(jnp.add, [x * w for (x, _), w in zip(items, shares)])
         result = (summed / total).astype(BF16)
         for j in range(GROUP):
             at = (g * GROUP + j) * HEAD_SIZE
@@ -276,19 +301,19 @@
     logits_ref[...] = logits
 
 
-def finish(queries, span_key_value, w_cand, sources, partials, width):
-    chains, span, _ = queries.shape
+def finish(shape, mine, w_cand, partials):
+    chains, span, _ = shape
     return pl.pallas_call(
-        functools.partial(finish_kernel, len(partials), width),
+        functools.partial(finish_kernel, chains, span),
         out_shape=(
-            jax.ShapeDtypeStruct(queries.shape, BF16),
+            jax.ShapeDtypeStruct(shape, BF16),
             jax.ShapeDtypeStruct((chains * span, NCAND), F32),
         ),
-        in_specs=[pl.BlockSpec(memory_space=VMEM)] * (3 + TEAM + len(partials)),
+        in_specs=[pl.BlockSpec(memory_space=VMEM)] * (3 + len(partials)),
         out_specs=(pl.BlockSpec(memory_space=VMEM),) * 2,
         compiler_params=params(),
-        cost_estimate=pl.CostEstimate(flops=1 << 27, bytes_accessed=1 << 20, transcendentals=0),
-    )(queries, span_key_value, w_cand, *sources, *partials)
+        cost_estimate=pl.CostEstimate(flops=1 << 24, bytes_accessed=1 << 20, transcendentals=0),
+    )(*mine, w_cand, *partials)
 
 
 def score_kernel(answer_ref, gathered_ref, score_ref, tally_ref):
@@ -343,17 +368,21 @@
         return lax.ppermute(array, "dp", [(i, i ^ offset) for i in range(owners)])
 
     offsets = range(1, TEAM)
-    jobs = [(j, 1, others) for j in offsets] + [(j, 0, 1) for j in offsets] + [(0, 1, others), (0, 0, 1)]
-    messages = pack(jobs, chains_here, owners, slot_tags, key_value_cache)
+    slot_tags = pltpu.with_memory_space_constraint(slot_tags, pltpu.HBM)
+    key_value_cache = pltpu.with_memory_space_constraint(key_value_cache, pltpu.HBM)
+    sort = functools.partial(pack, chains_here=chains_here, owners=owners, tags=slot_tags, cache=key_value_cache)
+    messages = sort([(j, 1, others) for j in offsets])
     far_in = [within(m, j) for m, j in zip(messages, offsets)]
     visiting = [across(queries, step) for step in range(1, teams)]
-    near_in = [within(m, j) for m, j in zip(messages[TEAM - 1 :], offsets)]
-    own_far, own_near = messages[-2:]
-    folded = fold(visiting, [own_far] + far_in, width)
+    mate = within(queries, DIAGONAL)
+    near = sort([(1, 0, 1), (2, 0, 1), (DIAGONAL, 0, 1), (0, 1, others), (0, 0, 1)])
+    near_in = [within(near[0], 1), within(near[1], 2)]
+    folded = fold(visiting, [near[3]] + far_in, width)
     partials = [across(m, teams - step) for m, step in zip(folded, range(1, teams))]
-    attended, partial_logits = finish(
-        queries, span_key_value, w_cand, [own_near] + near_in, partials, width
-    )
+    answer = fold([mate], [near[2]], width)
+    partials = [within(answer[0], DIAGONAL)] + partials
+    mine = own(queries, span_key_value, [near[4]] + near_in, width)
+    attended, partial_logits = finish(queries.shape, mine, w_cand, partials)
     gathered = lax.all_gather(partial_logits, "mp")
     prompts = owners * chains_here // SAMPLES
     scores, tally = score(gathered, answer_id, prompts)

time: 59.3 us -> 55 us (0.927)
  waiting for transfers between devices: 24.1 us -> 15.6 us
  starting transfers between devices: 19.8 us -> 22.4 us
  Pallas kernels: 7.27 us -> 9.51 us
  local copies, waits for them, and re-layouts: 1.92 us -> 1.23 us
    ppermute x2, waiting for transfers between devices: 8.55 us -> 0.01 us  [across(): return lax.ppermute(array, 'dp', pairs)]
    ppermute x9 -> x10, starting transfers between devices: 14.9 us -> 17.4 us  [within(): return lax.ppermute(array, 'dp', [(i, i ^ offset) for i in range(owners)])]
    pallas_call x1 -> x2, Pallas kernels: 2.79 us -> 5.02 us  [pack(): pl.pallas_call(functools.partial(pack_kernel, jobs, chains_here, owners),...]
    unnamed x10 -> x8, local copies, waits for them, and re-layouts: 0.71 us -> 0.02 us
    ppermute x9 -> x10, waiting for transfers between devices: 15.5 us -> 15.6 us  [within(): return lax.ppermute(array, 'dp', [(i, i ^ offset) for i in range(owners)])]
    pallas_call x2 -> x4, Pallas kernels: 3.76 us -> 3.77 us  [the longest x2 1.69 us: fold(): pl.pallas_call(functools.partial(fold_kernel, classes, held, width), out_...]
  transfers between devices with their start and end apart: 11 -> 12, of which waited for: 6 -> 6; matrix products, arithmetic and copies ran while one was open for 1% -> 1% of each run, Pallas kernels for 2% -> 10%
where the time goes in v1:
time: 55 us; the launch traced here: 54.7 us
  starting transfers between devices  22.4 us (41%)
  waiting for transfers between devices  15.6 us (28%)
  Pallas kernels  9.51 us (17%)
  blocking collectives  5.22 us (9%)
  local copies, waits for them, and re-layouts  1.23 us (2%)
  between operations  0.74 us (1%)
    ppermute x10, starting transfers between devices, within(): return lax.ppermute(array, 'dp', [(i, i ^ offset) for i in range(owners)])  17.4 us
    ppermute x10, waiting for transfers between devices, within(): return lax.ppermute(array, 'dp', [(i, i ^ offset) for i in range(owners)])  15.6 us
    all_gather x1, blocking collectives, program(): gathered = lax.all_gather(partial_logits, 'mp')  5.22 us
    pallas_call x2, Pallas kernels, pack(): pl.pallas_call(functools.partial(pack_kernel, jobs, chains_here, owners),...  5.02 us
    ppermute x2, starting transfers between devices, across(): return lax.ppermute(array, 'dp', pairs)  5.02 us
    pallas_call x2, Pallas kernels, fold(): pl.pallas_call(functools.partial(fold_kernel, classes, held, width), out_...  1.69 us
  transfers between devices with their start and end apart: 12, of which 6 were waited for; matrix products, arithmetic and copies ran while one was open for 1% of the time, Pallas kernels for 10%

profile of v1, /device:TPU:0, one launch (start us, length us, event | category | flops | bytes accessed | tf_op | source)
XLA Modules:
  0.0 54.7 jit_solution(5415924033459708310)
XLA Ops:
  0.6 0.0 copy-start.1
  0.6 2.5 %shard_map.88 = (bf16[520,256]{1,0:T(8,128)(2,1)S(1)}, bf16[520,256]{1,0:T(8,128)(2,1)S(1)}, bf16[520,256]{1,0:T(8,128)(2,1)S(1)}) custom-call(s32[16]{0:T(128)} %tags_hbm.3, bf16[16,2,128,256]{3,2,1,0:T(8,128)(2,1)} %cache_ref.3), custom_call_target="tpu_custom_call" | custom-call | bytes 1597440 | tf_op jit(solution)/shard_map/pallas_call | solution.py:105
  3.1 0.0 copy-start.2
  3.1 3.0 %collective-permute-start.5 = (bf16[520,256]{1,0:T(8,128)(2,1)S(1)}, bf16[520,256]{1,0:T(8,128)(2,1)S(1)}, u32[]{:S(2)}, u32[]{:S(2)}) collective-permute-start(bf16[520,256]{1,0:T(8,128)(2,1)S(1)} %get-tuple-element.24), channel_id=1, source_target_pairs={{0,4},{4,0},{8,12},{12,8},{16,20},{20,16},{24,28},{28,24},{1,5},{5... | collective-permute-start | bytes 798728 | tf_op jit(solution)/shard_map/ppermute | solution.py:368
  6.2 1.6 %collective-permute-start.6 = (bf16[520,256]{1,0:T(8,128)(2,1)S(1)}, bf16[520,256]{1,0:T(8,128)(2,1)S(1)}, u32[]{:S(2)}, u32[]{:S(2)}) collective-permute-start(bf16[520,256]{1,0:T(8,128)(2,1)S(1)} %get-tuple-element.25), channel_id=1, source_target_pairs={{0,8},{4,12},{8,0},{12,4},{16,24},{20,28},{24,16},{28,20},{1,9},{5... | collective-permute-start | bytes 798728 | tf_op jit(solution)/shard_map/ppermute | solution.py:368
  7.7 0.0 copy-start
  7.7 0.0 collective-permute-start.7
  7.7 0.0 copy-done.1
  7.7 2.9 %collective-permute-start.2 = (bf16[2,16,1280]{2,1,0:T(8,128)(2,1)S(1)}, bf16[2,16,1280]{2,1,0:T(8,128)(2,1)S(1)}, u32[]{:S(2)}, u32[]{:S(2)}) collective-permute-start(bf16[2,16,1280]{2,1,0:T(8,128)(2,1)S(1)} %copy-done.1), channel_id=1, source_target_pairs={{0,12},{4,8},{8,4},{12,0},{16,28},{20,24},{24,20},{28,16},{1,13},{... | collective-permute-start | bytes 245768 | tf_op jit(solution)/shard_map/ppermute | solution.py:368
  10.7 2.6 %collective-permute-start.4 = (bf16[2,16,1280]{2,1,0:T(8,128)(2,1)S(1)}, bf16[2,16,1280]{2,1,0:T(8,128)(2,1)S(1)}, u32[]{:S(2)}, u32[]{:S(2)}) collective-permute-start(bf16[2,16,1280]{2,1,0:T(8,128)(2,1)S(1)} %copy-done.1), channel_id=1, source_target_pairs={{16,0},{20,4},{24,8},{28,12},{0,16},{4,20},{8,24},{12,28},{17,1},{... | collective-permute-start | bytes 245768 | tf_op jit(solution)/shard_map/ppermute | solution.py:365
  13.3 2.6 %shard_map.85 = (bf16[520,256]{1,0:T(8,128)(2,1)S(1)}, bf16[520,256]{1,0:T(8,128)(2,1)S(1)}, bf16[520,256]{1,0:T(8,128)(2,1)S(1)}, bf16[520,256]{1,0:T(8,128)(2,1)S(1)}, bf16[520,256]{1,0:T(8,128)(2,1)S(1)}) custom-call(s32[16]{0:T(128)} %tags_hbm.3, bf16[16,2,128,256]{3,2,1,0:T(8,128)(2,1)} %cache_ref.3), custom_call_target="tpu_custom_call" | custom-call | bytes 2662400 | tf_op jit(solution)/shard_map/pallas_call | solution.py:105
  15.8 0.0 copy-start.3
  15.8 7.2 %collective-permute-done.2.refs_0_ = bf16[2,16,1280]{2,1,0:T(8,128)(2,1)S(1)} collective-permute-done((bf16[2,16,1280]{2,1,0:T(8,128)(2,1)S(1)}, bf16[2,16,1280]{2,1,0:T(8,128)(2,1)S(1)}, u32[]{:S(2)}, u32[]{:S(2)}) %collective-permute-start.2) | collective-permute-done | bytes 81952 | tf_op jit(solution)/shard_map/ppermute | solution.py:368
  23.0 1.7 %collective-permute-start = (bf16[520,256]{1,0:T(8,128)(2,1)S(1)}, bf16[520,256]{1,0:T(8,128)(2,1)S(1)}, u32[]{:S(2)}, u32[]{:S(2)}) collective-permute-start(bf16[520,256]{1,0:T(8,128)(2,1)S(1)} %get-tuple-element.18), channel_id=1, source_target_pairs={{0,4},{4,0},{8,12},{12,8},{16,20},{20,16},{24,28},{28,24},{1,5},{5... | collective-permute-start | bytes 798728 | tf_op jit(solution)/shard_map/ppermute | solution.py:368
  24.7 0.0 collective-permute-done.4.refs_0_
  24.7 1.1 %collective-permute-start.1 = (bf16[520,256]{1,0:T(8,128)(2,1)S(1)}, bf16[520,256]{1,0:T(8,128)(2,1)S(1)}, u32[]{:S(2)}, u32[]{:S(2)}) collective-permute-start(bf16[520,256]{1,0:T(8,128)(2,1)S(1)} %get-tuple-element.19), channel_id=1, source_target_pairs={{0,8},{4,12},{8,0},{12,4},{16,24},{20,28},{24,16},{28,20},{1,9},{5... | collective-permute-start | bytes 798728 | tf_op jit(solution)/shard_map/ppermute | solution.py:368
  25.8 0.5 shard_map.87
  26.3 0.0 collective-permute-done.5.refs_2_
  26.3 0.8 %collective-permute-start.3 = (bf16[336,128]{1,0:T(8,128)(2,1)S(1)}, bf16[336,128]{1,0:T(8,128)(2,1)S(1)}, u32[]{:S(2)}, u32[]{:S(2)}) collective-permute-start(bf16[336,128]{1,0:T(8,128)(2,1)S(1)} %shard_map.87), channel_id=1, source_target_pairs={{0,12},{4,8},{8,4},{12,0},{16,28},{20,24},{24,20},{28,16},{1,13},{... | collective-permute-start | bytes 258056 | tf_op jit(solution)/shard_map/ppermute | solution.py:368
  27.1 0.0 collective-permute-done.6.refs_3_
  27.1 0.0 collective-permute-done.7.refs_4_
  27.1 1.2 %shard_map.89 = bf16[336,128]{1,0:T(8,128)(2,1)S(1)} custom-call(bf16[2,16,1280]{2,1,0:T(8,128)(2,1)S(1)} %collective-permute-done.4.refs_0_, bf16[520,256]{1,0:T(8,128)(2,1)S(1)} %get-tuple-element.23.refs_1_, bf16[520,256]{1,0:T(8,128)(2,1)S(1)} %collective-permute-done.5.refs_2_, bf16[520,256]{1,0:T(8,128)(2,1)S(1)} %collective-permute-done.6.refs_3_, ...), custom_call_target="tpu_custom_call" | custom-call | flops 167772160 | bytes 1048576 | tf_op jit(solution)/shard_map/pallas_call | solution.py:215
  28.3 2.4 %collective-permute-start.8 = (bf16[336,128]{1,0:T(8,128)(2,1)S(1)}, bf16[336,128]{1,0:T(8,128)(2,1)S(1)}, u32[]{:S(2)}, u32[]{:S(2)}) collective-permute-start(bf16[336,128]{1,0:T(8,128)(2,1)S(1)} %shard_map.89), channel_id=1, source_target_pairs={{16,0},{20,4},{24,8},{28,12},{0,16},{4,20},{8,24},{12,28},{17,1},{... | collective-permute-start | bytes 258056 | tf_op jit(solution)/shard_map/ppermute | solution.py:365
  30.7 0.4 collective-permute-done.refs_3_
  31.2 2.5 %collective-permute-done.1.refs_4_ = bf16[520,256]{1,0:T(8,128)(2,1)S(1)} collective-permute-done((bf16[520,256]{1,0:T(8,128)(2,1)S(1)}, bf16[520,256]{1,0:T(8,128)(2,1)S(1)}, u32[]{:S(2)}, u32[]{:S(2)}) %collective-permute-start.1) | collective-permute-done | bytes 266272 | tf_op jit(solution)/shard_map/ppermute | solution.py:368
  33.7 0.0 copy-done.2
  33.7 1.1 %shard_map.86 = (f32[320,128]{1,0:T(8,128)S(1)}, f32[320,128]{1,0:T(8,128)S(1)}) custom-call(bf16[2,16,1280]{2,1,0:T(8,128)(2,1)S(1)} %copy-done.1, bf16[2,2,16,256]{3,2,1,0:T(8,128)(2,1)S(1)} %copy-done.2, bf16[520,256]{1,0:T(8,128)(2,1)S(1)} %get-tuple-element.17.refs_2_, bf16[520,256]{1,0:T(8,128)(2,1)S(1)} %collective-permute-done.refs_3_, ...), custom_call_target="tpu_custom_call" | custom-call | flops 125829120 | bytes 1048576 | tf_op jit(solution)/shard_map/pallas_call | solution.py:255
  34.8 0.0 collective-permute-done.3.refs_3_
  34.8 0.0 collective-permute-done.8.refs_4_
  34.8 0.0 copy-done
  34.8 1.0 %shard_map.90 = (bf16[2,16,1280]{2,1,0:T(8,128)(2,1)}, f32[32,128]{1,0:T(8,128)S(1)}) custom-call(f32[320,128]{1,0:T(8,128)S(1)} %get-tuple-element.20.refs_0_, f32[320,128]{1,0:T(8,128)S(1)} %get-tuple-element.21.refs_1_, bf16[1280,128]{1,0:T(8,128)(2,1)S(1)} %copy-done, bf16[336,128]{1,0:T(8,128)(2,1)S(1)} %collective-permute-done.3.refs_3_, ...), custom_call_target="tpu_custom_call" | custom-call | flops 16777216 | bytes 1048576 | tf_op jit(solution)/shard_map/pallas_call | solution.py:306
  35.8 5.2 %all-gather = f32[128,128]{1,0:T(8,128)S(1)} all-gather(f32[32,128]{1,0:T(8,128)S(1)} %get-tuple-element.28), channel_id=2, replica_groups=mesh['dp'=8,'mp'=4] {'mp'}, dimensions={0}, use_global_device_ids=true | all-gather | bytes 81920 | tf_op jit(solution)/shard_map/all_gather | solution.py:386
  41.0 0.0 copy-done.3
  41.0 0.7 %shard_map.91 = (f32[2,128]{1,0:T(2,128)S(1)}, f32[1,128]{1,0:T(1,128)S(1)}) custom-call(s32[2]{0:T(128)S(1)} %copy-done.3, f32[4,32,128]{2,1,0:T(8,128)S(1)} %bitcast.1), custom_call_target="tpu_custom_call" | custom-call | flops 1048576 | bytes 65536 | tf_op jit(solution)/shard_map/pallas_call | solution.py:343
  41.7 1.8 %collective-permute-start.9 = (f32[1,128]{1,0:T(1,128)S(1)}, f32[1,128]{1,0:T(1,128)S(1)}, u32[]{:S(2)}, u32[]{:S(2)}) collective-permute-start(f32[1,128]{1,0:T(1,128)S(1)} %get-tuple-element.30), channel_id=1, source_target_pairs={{0,4},{4,0},{8,12},{12,8},{16,20},{20,16},{24,28},{28,24},{1,5},{5... | collective-permute-start | bytes 1544 | tf_op jit(solution)/shard_map/ppermute | solution.py:368
  43.6 1.8 %collective-permute-done.9 = f32[1,128]{1,0:T(1,128)S(1)} collective-permute-done((f32[1,128]{1,0:T(1,128)S(1)}, f32[1,128]{1,0:T(1,128)S(1)}, u32[]{:S(2)}, u32[]{:S(2)}) %collective-permute-start.9) | collective-permute-done | bytes 544 | tf_op jit(solution)/shard_map/ppermute | solution.py:368
  45.4 2.7 %collective-permute-start.10 = (f32[1,128]{1,0:T(1,128)S(1)}, f32[1,128]{1,0:T(1,128)S(1)}, u32[]{:S(2)}, u32[]{:S(2)}) collective-permute-start(f32[1,128]{1,0:T(1,128)S(1)} %add.12), channel_id=1, source_target_pairs={{0,8},{4,12},{8,0},{12,4},{16,24},{20,28},{24,16},{28,20},{1,9},{5... | collective-permute-start | bytes 1544 | tf_op jit(solution)/shard_map/ppermute | solution.py:368
  48.1 1.5 %collective-permute-done.10 = f32[1,128]{1,0:T(1,128)S(1)} collective-permute-done((f32[1,128]{1,0:T(1,128)S(1)}, f32[1,128]{1,0:T(1,128)S(1)}, u32[]{:S(2)}, u32[]{:S(2)}) %collective-permute-start.10) | collective-permute-done | bytes 544 | tf_op jit(solution)/shard_map/ppermute | solution.py:368
  49.6 1.7 %collective-permute-start.11 = (f32[1,128]{1,0:T(1,128)S(1)}, f32[1,128]{1,0:T(1,128)S(1)}, u32[]{:S(2)}, u32[]{:S(2)}) collective-permute-start(f32[1,128]{1,0:T(1,128)S(1)} %add.13), channel_id=1, source_target_pairs={{0,16},{4,20},{8,24},{12,28},{16,0},{20,4},{24,8},{28,12},{1,17},{... | collective-permute-start | bytes 1544 | tf_op jit(solution)/shard_map/ppermute | solution.py:368
  51.4 0.6 %slice_reduce_fusion = f32[2]{0:T(128)} fusion(f32[2,128]{1,0:T(2,128)S(1)} %get-tuple-element.29), kind=kLoop, calls=%fused_computation | loop fusion | bytes 16 | tf_op jit(solution)/shard_map/slice | solution.py:389
  52.0 2.1 %collective-permute-done.11 = f32[1,128]{1,0:T(1,128)S(1)} collective-permute-done((f32[1,128]{1,0:T(1,128)S(1)}, f32[1,128]{1,0:T(1,128)S(1)}, u32[]{:S(2)}, u32[]{:S(2)}) %collective-permute-start.11) | collective-permute-done | bytes 544 | tf_op jit(solution)/shard_map/ppermute | solution.py:368
  54.1 0.6 %constant_dynamic-slice_fusion = f32[1,16]{1,0:T(1,128)} fusion(f32[1,128]{1,0:T(1,128)S(1)} %add.14, s32[]{:T(128)S(6)} %select_n.3), kind=kLoop, calls=%fused_computation.1 | loop fusion | bytes 132 | tf_op jit(solution)/shard_map/dynamic_slice | solution.py:395
  (3 shorter events, 0.0 us)
Async XLA Ops:
  0.6 7.1 %copy-start.1 = (bf16[2,16,1280]{2,1,0:T(8,128)(2,1)S(1)}, bf16[2,16,1280]{2,1,0:T(8,128)(2,1)}, u32[]{:S(2)}) copy-start(bf16[2,16,1280]{2,1,0:T(8,128)(2,1)} %refs_0_.1) | copy-start | bytes 245764
  3.1 30.6 %copy-start.2 = (bf16[2,2,16,256]{3,2,1,0:T(8,128)(2,1)S(1)}, bf16[2,2,16,256]{3,2,1,0:T(8,128)(2,1)}, u32[]{:S(2)}) copy-start(bf16[2,2,16,256]{3,2,1,0:T(8,128)(2,1)} %refs_1_.1) | copy-start | bytes 98308
  3.1 23.2 %collective-permute-start.5 = (bf16[520,256]{1,0:T(8,128)(2,1)S(1)}, bf16[520,256]{1,0:T(8,128)(2,1)S(1)}, u32[]{:S(2)}, u32[]{:S(2)}) collective-permute-start(bf16[520,256]{1,0:T(8,128)(2,1)S(1)} %get-tuple-element.24), channel_id=1, source_target_pairs={{0,4},{4,0},{8,12},{12,8},{16,20},{20,16},{24,28},{28,24},{1,5},{5... | collective-permute-start | bytes 798728 | tf_op jit(solution)/shard_map/ppermute | solution.py:368
  6.2 20.9 %collective-permute-start.6 = (bf16[520,256]{1,0:T(8,128)(2,1)S(1)}, bf16[520,256]{1,0:T(8,128)(2,1)S(1)}, u32[]{:S(2)}, u32[]{:S(2)}) collective-permute-start(bf16[520,256]{1,0:T(8,128)(2,1)S(1)} %get-tuple-element.25), channel_id=1, source_target_pairs={{0,8},{4,12},{8,0},{12,4},{16,24},{20,28},{24,16},{28,20},{1,9},{5... | collective-permute-start | bytes 798728 | tf_op jit(solution)/shard_map/ppermute | solution.py:368
  7.7 27.1 %copy-start = (bf16[1280,128]{1,0:T(8,128)(2,1)S(1)}, bf16[1280,128]{1,0:T(8,128)(2,1)}, u32[]{:S(2)}) copy-start(bf16[1280,128]{1,0:T(8,128)(2,1)} %refs_2_.1) | copy-start | bytes 983044
  7.7 19.4 %collective-permute-start.7 = (bf16[520,256]{1,0:T(8,128)(2,1)S(1)}, bf16[520,256]{1,0:T(8,128)(2,1)S(1)}, u32[]{:S(2)}, u32[]{:S(2)}) collective-permute-start(bf16[520,256]{1,0:T(8,128)(2,1)S(1)} %get-tuple-element.26), channel_id=1, source_target_pairs={{0,12},{4,8},{8,4},{12,0},{16,28},{20,24},{24,20},{28,16},{1,13},{... | collective-permute-start | bytes 798728 | tf_op jit(solution)/shard_map/ppermute | solution.py:368
  7.7 15.3 %collective-permute-start.2 = (bf16[2,16,1280]{2,1,0:T(8,128)(2,1)S(1)}, bf16[2,16,1280]{2,1,0:T(8,128)(2,1)S(1)}, u32[]{:S(2)}, u32[]{:S(2)}) collective-permute-start(bf16[2,16,1280]{2,1,0:T(8,128)(2,1)S(1)} %copy-done.1), channel_id=1, source_target_pairs={{0,12},{4,8},{8,4},{12,0},{16,28},{20,24},{24,20},{28,16},{1,13},{... | collective-permute-start | bytes 245768 | tf_op jit(solution)/shard_map/ppermute | solution.py:368
  10.7 14.0 %collective-permute-start.4 = (bf16[2,16,1280]{2,1,0:T(8,128)(2,1)S(1)}, bf16[2,16,1280]{2,1,0:T(8,128)(2,1)S(1)}, u32[]{:S(2)}, u32[]{:S(2)}) collective-permute-start(bf16[2,16,1280]{2,1,0:T(8,128)(2,1)S(1)} %copy-done.1), channel_id=1, source_target_pairs={{16,0},{20,4},{24,8},{28,12},{0,16},{4,20},{8,24},{12,28},{17,1},{... | collective-permute-start | bytes 245768 | tf_op jit(solution)/shard_map/ppermute | solution.py:365
  15.8 25.2 %copy-start.3 = (s32[2]{0:T(128)S(1)}, s32[2]{0:T(128)}, u32[]{:S(2)}) copy-start(s32[2]{0:T(128)} %answer_ref.1) | copy-start | bytes 28
  23.0 8.1 %collective-permute-start = (bf16[520,256]{1,0:T(8,128)(2,1)S(1)}, bf16[520,256]{1,0:T(8,128)(2,1)S(1)}, u32[]{:S(2)}, u32[]{:S(2)}) collective-permute-start(bf16[520,256]{1,0:T(8,128)(2,1)S(1)} %get-tuple-element.18), channel_id=1, source_target_pairs={{0,4},{4,0},{8,12},{12,8},{16,20},{20,16},{24,28},{28,24},{1,5},{5... | collective-permute-start | bytes 798728 | tf_op jit(solution)/shard_map/ppermute | solution.py:368
  24.7 9.0 %collective-permute-start.1 = (bf16[520,256]{1,0:T(8,128)(2,1)S(1)}, bf16[520,256]{1,0:T(8,128)(2,1)S(1)}, u32[]{:S(2)}, u32[]{:S(2)}) collective-permute-start(bf16[520,256]{1,0:T(8,128)(2,1)S(1)} %get-tuple-element.19), channel_id=1, source_target_pairs={{0,8},{4,12},{8,0},{12,4},{16,24},{20,28},{24,16},{28,20},{1,9},{5... | collective-permute-start | bytes 798728 | tf_op jit(solution)/shard_map/ppermute | solution.py:368
  26.3 8.5 %collective-permute-start.3 = (bf16[336,128]{1,0:T(8,128)(2,1)S(1)}, bf16[336,128]{1,0:T(8,128)(2,1)S(1)}, u32[]{:S(2)}, u32[]{:S(2)}) collective-permute-start(bf16[336,128]{1,0:T(8,128)(2,1)S(1)} %shard_map.87), channel_id=1, source_target_pairs={{0,12},{4,8},{8,4},{12,0},{16,28},{20,24},{24,20},{28,16},{1,13},{... | collective-permute-start | bytes 258056 | tf_op jit(solution)/shard_map/ppermute | solution.py:368
  28.3 6.5 %collective-permute-start.8 = (bf16[336,128]{1,0:T(8,128)(2,1)S(1)}, bf16[336,128]{1,0:T(8,128)(2,1)S(1)}, u32[]{:S(2)}, u32[]{:S(2)}) collective-permute-start(bf16[336,128]{1,0:T(8,128)(2,1)S(1)} %shard_map.89), channel_id=1, source_target_pairs={{16,0},{20,4},{24,8},{28,12},{0,16},{4,20},{8,24},{12,28},{17,1},{... | collective-permute-start | bytes 258056 | tf_op jit(solution)/shard_map/ppermute | solution.py:365
  41.7 3.6 %collective-permute-start.9 = (f32[1,128]{1,0:T(1,128)S(1)}, f32[1,128]{1,0:T(1,128)S(1)}, u32[]{:S(2)}, u32[]{:S(2)}) collective-permute-start(f32[1,128]{1,0:T(1,128)S(1)} %get-tuple-element.30), channel_id=1, source_target_pairs={{0,4},{4,0},{8,12},{12,8},{16,20},{20,16},{24,28},{28,24},{1,5},{5... | collective-permute-start | bytes 1544 | tf_op jit(solution)/shard_map/ppermute | solution.py:368
  45.4 4.3 %collective-permute-start.10 = (f32[1,128]{1,0:T(1,128)S(1)}, f32[1,128]{1,0:T(1,128)S(1)}, u32[]{:S(2)}, u32[]{:S(2)}) collective-permute-start(f32[1,128]{1,0:T(1,128)S(1)} %add.12), channel_id=1, source_target_pairs={{0,8},{4,12},{8,0},{12,4},{16,24},{20,28},{24,16},{28,20},{1,9},{5... | collective-permute-start | bytes 1544 | tf_op jit(solution)/shard_map/ppermute | solution.py:368
  49.6 4.5 %collective-permute-start.11 = (f32[1,128]{1,0:T(1,128)S(1)}, f32[1,128]{1,0:T(1,128)S(1)}, u32[]{:S(2)}, u32[]{:S(2)}) collective-permute-start(f32[1,128]{1,0:T(1,128)S(1)} %add.13), channel_id=1, source_target_pairs={{0,16},{4,20},{8,24},{12,28},{16,0},{20,4},{24,8},{28,12},{1,17},{... | collective-permute-start | bytes 1544 | tf_op jit(solution)/shard_map/ppermute | solution.py:368

commit v2 on v1

--- a/solution.py
+++ b/solution.py
@@ -18,6 +18,7 @@
 LANES = 128
 TEAM = 4
 DIAGONAL = 3
+PULLS = 4
 BIG_NEG = -1e30
 
 
@@ -39,35 +40,34 @@
 
 
 def find_slots(tags_ref, slot_ref, count_ref, chains_here, owners):
-    def clear(o, _):
+    for o in range(owners):
         count_ref[o] = 0
         for k in range(PEER):
             slot_ref[o * PEER + k] = -1
-        return 0
-
-    lax.fori_loop(0, owners, clear, 0)
-
-    def place(s, _):
-        owner = tags_ref[s] // chains_here
+    for s in range(tags_ref.shape[0]):
+        owner = lax.div(tags_ref[s], chains_here)
         rank = jnp.minimum(count_ref[owner], PEER - 1)
         slot_ref[owner * PEER + rank] = s
         count_ref[owner] = rank + 1
-        return 0
-
-    lax.fori_loop(0, tags_ref.shape[0], place, 0)
-
-
-def pack_kernel(jobs, chains_here, owners, tags_hbm, cache_ref, *refs):
+
+
+def pack_kernel(jobs, chains_here, owners, tags_hbm, cache_hbm, *refs):
     outs = refs[: len(jobs)]
-    tags_ref, slot_ref, count_ref, tag_sem, sem = refs[len(jobs) :]
-    width = cache_ref.shape[2]
+    cache_ref, tags_ref, slot_ref, count_ref, tag_sem, sem = refs[len(jobs) :]
     fetch = pltpu.make_async_copy(tags_hbm, tags_ref, tag_sem)
     fetch.start()
+    slots, length = cache_ref.shape[:2]
+    step = -(-slots // sem.shape[0])
+    pulls = []
+    for i, at in enumerate(range(0, slots, step)):
+        here = pl.ds(at, min(step, slots - at))
+        pulls.append(pltpu.make_async_copy(cache_hbm.at[here], cache_ref.at[here], sem.at[i]))
+        pulls[-1].start()
     position = lax.axis_index("dp")
-    row, high, high_count = lax.rem(position, TEAM), position // TEAM, owners // TEAM
+    row, high, high_count = lax.rem(position, TEAM), lax.div(position, TEAM), owners // TEAM
     fetch.wait()
     find_slots(tags_ref, slot_ref, count_ref, chains_here, owners)
-    copies = []
+    picks = []
     for out, (offset, first, classes) in zip(outs, jobs):
         member = row ^ offset
         blocks = classes * PEER
@@ -78,44 +78,38 @@
             for k in range(PEER):
                 slot = slot_ref[owner * PEER + k]
                 safe = jnp.maximum(slot, 0)
-                chain = jnp.where(slot < 0, chains_here, tags_ref[safe] % chains_here)
+                chain = jnp.where(slot < 0, chains_here, lax.rem(tags_ref[safe], chains_here))
                 index = h * PEER + k
-                for part in range(2):
-                    copy = pltpu.make_async_copy(
-                        cache_ref.at[safe, part],
-                        out.at[pl.ds((index * 2 + part) * width, width)],
-                        sem.at[len(copies)],
-                    )
-                    copy.start()
-                    copies.append(copy)
                 note = jnp.where(line == index, chain.astype(F32), note)
-        out[pl.ds(blocks * 2 * width, note_rows(blocks)), :] = note.astype(BF16)
-    for copy in copies:
-        copy.wait()
+                picks.append((out, index, safe))
+        out[pl.ds(blocks * length, note_rows(blocks)), :] = note.astype(BF16)
+    for pull in pulls:
+        pull.wait()
+    for out, index, safe in picks:
+        out[pl.ds(index * length, length), :] = cache_ref[safe]
 
 
 def pack(jobs, chains_here, owners, tags, cache):
-    width, lanes = cache.shape[2], cache.shape[3]
+    _, length, lanes = cache.shape
     shapes = []
     for _, _, classes in jobs:
         blocks = classes * PEER
-        shapes.append(jax.ShapeDtypeStruct((blocks * 2 * width + note_rows(blocks), lanes), BF16))
-    moved = sum(s.shape[0] * s.shape[1] * 2 for s in shapes)
-    count = sum(classes * PEER * 2 for _, _, classes in jobs)
+        shapes.append(jax.ShapeDtypeStruct((blocks * length + note_rows(blocks), lanes), BF16))
     return pl.pallas_call(
         functools.partial(pack_kernel, jobs, chains_here, owners),
         out_shape=tuple(shapes),
         in_specs=[pl.BlockSpec(memory_space=pltpu.HBM)] * 2,
         out_specs=tuple(pl.BlockSpec(memory_space=VMEM) for _ in jobs),
         scratch_shapes=[
+            VMEM(cache.shape, BF16),
             pltpu.SMEM(tags.shape, jnp.int32),
             pltpu.SMEM((owners * PEER,), jnp.int32),
             pltpu.SMEM((owners,), jnp.int32),
             pltpu.SemaphoreType.DMA,
-            pltpu.SemaphoreType.DMA((count,)),
+            pltpu.SemaphoreType.DMA((PULLS,)),
         ],
         compiler_params=params(),
-        cost_estimate=pl.CostEstimate(flops=0, bytes_accessed=2 * moved, transcendentals=0),
+        cost_estimate=pl.CostEstimate(flops=0, bytes_accessed=cache.size * 2, transcendentals=0),
     )(tags, cache)
 
 
@@ -367,21 +361,31 @@
     def within(array, offset):
         return lax.ppermute(array, "dp", [(i, i ^ offset) for i in range(owners)])
 
-    offsets = range(1, TEAM)
+    def crosswise(array, step):
+        pairs = [
+            (((t + step) % teams) * TEAM + (r ^ DIAGONAL), t * TEAM + r) for t in range(teams) for r in range(TEAM)
+        ]
+        return lax.ppermute(array, "dp", pairs)
+
+    key_value_cache = key_value_cache.reshape(key_value_cache.shape[0], 2 * width, -1)
     slot_tags = pltpu.with_memory_space_constraint(slot_tags, pltpu.HBM)
     key_value_cache = pltpu.with_memory_space_constraint(key_value_cache, pltpu.HBM)
-    sort = functools.partial(pack, chains_here=chains_here, owners=owners, tags=slot_tags, cache=key_value_cache)
-    messages = sort([(j, 1, others) for j in offsets])
-    far_in = [within(m, j) for m, j in zip(messages, offsets)]
+    jobs = [(1, 1, others), (2, 1, others), (0, 1, others), (1, 0, 1), (2, 0, 1), (0, 0, 1), (DIAGONAL, 0, teams)]
+    messages = pack(jobs, chains_here, owners, slot_tags, key_value_cache)
+    far_in, near_in = [], []
+    for j in (1, 2):
+        far_in.append(within(messages[j - 1], j))
     visiting = [across(queries, step) for step in range(1, teams)]
-    mate = within(queries, DIAGONAL)
-    near = sort([(1, 0, 1), (2, 0, 1), (DIAGONAL, 0, 1), (0, 1, others), (0, 0, 1)])
-    near_in = [within(near[0], 1), within(near[1], 2)]
-    folded = fold(visiting, [near[3]] + far_in, width)
+    mates = [within(queries, DIAGONAL)]
+    mates += [crosswise(queries, step) for step in range(1, teams)]
+    for j in (1, 2):
+        near_in.append(within(messages[j + 2], j))
+    folded = fold(visiting, [messages[2]] + far_in, width)
     partials = [across(m, teams - step) for m, step in zip(folded, range(1, teams))]
-    answer = fold([mate], [near[2]], width)
-    partials = [within(answer[0], DIAGONAL)] + partials
-    mine = own(queries, span_key_value, [near[4]] + near_in, width)
+    answers = fold(mates, [messages[6]], width)
+    partials.append(within(answers[0], DIAGONAL))
+    partials += [crosswise(m, teams - step) for m, step in zip(answers[1:], range(1, teams))]
+    mine = own(queries, span_key_value, [messages[5]] + near_in, width)
     attended, partial_logits = finish(queries.shape, mine, w_cand, partials)
     gathered = lax.all_gather(partial_logits, "mp")
     prompts = owners * chains_here // SAMPLES

time: 55 us -> 60.4 us (1.098)
  waiting for transfers between devices: 15.6 us -> 28.1 us
  starting transfers between devices: 22.4 us -> 18.3 us
  Pallas kernels: 9.51 us -> 6.72 us
    ppermute x10 -> x9, starting transfers between devices: 17.4 us -> 9.54 us  [within(): return lax.ppermute(array, 'dp', [(i, i ^ offset) for i in range(owners)])]
    ppermute x2, waiting for transfers between devices: 0.01 us -> 7.44 us  [across(): return lax.ppermute(array, 'dp', pairs)]
    ppermute x0 -> x2, starting transfers between devices: none -> 7.35 us  [crosswise(): return lax.ppermute(array, 'dp', pairs)]
    ppermute x0 -> x2, waiting for transfers between devices: none -> 4.89 us  [crosswise(): return lax.ppermute(array, 'dp', pairs)]
    ppermute x2, starting transfers between devices: 5.02 us -> 1.39 us  [across(): return lax.ppermute(array, 'dp', pairs)]
    pallas_call x2 -> x1, Pallas kernels: 5.02 us -> 1.75 us  [pack(): pl.pallas_call(functools.partial(pack_kernel, jobs, chains_here, owners),...]
    ppermute x10 -> x9, waiting for transfers between devices: 15.6 us -> 15.8 us  [within(): return lax.ppermute(array, 'dp', [(i, i ^ offset) for i in range(owners)])]
  transfers between devices with their start and end apart: 12 -> 13, of which waited for: 6 -> 8; matrix products, arithmetic and copies ran while one was open for 1% -> 1% of each run, Pallas kernels for 10% -> 5%
where the time goes in v2:
time: 60.4 us; the launch traced here: 60.3 us
  waiting for transfers between devices  28.1 us (47%)
  starting transfers between devices  18.3 us (30%)
  Pallas kernels  6.72 us (11%)
  blocking collectives  5.22 us (9%)
  local copies, waits for them, and re-layouts  1.23 us (2%)
  between operations  0.74 us (1%)
    ppermute x9, waiting for transfers between devices, within(): return lax.ppermute(array, 'dp', [(i, i ^ offset) for i in range(owners)])  15.8 us
    ppermute x9, starting transfers between devices, within(): return lax.ppermute(array, 'dp', [(i, i ^ offset) for i in range(owners)])  9.54 us
    ppermute x2, waiting for transfers between devices, across(): return lax.ppermute(array, 'dp', pairs)  7.44 us
    ppermute x2, starting transfers between devices, crosswise(): return lax.ppermute(array, 'dp', pairs)  7.35 us
    all_gather x1, blocking collectives, program(): gathered = lax.all_gather(partial_logits, 'mp')  5.22 us
    ppermute x2, waiting for transfers between devices, crosswise(): return lax.ppermute(array, 'dp', pairs)  4.89 us
    pallas_call x2, Pallas kernels, fold(): pl.pallas_call(functools.partial(fold_kernel, classes, held, width), out_...  2.08 us
    pallas_call x1, Pallas kernels, pack(): pl.pallas_call(functools.partial(pack_kernel, jobs, chains_here, owners),...  1.75 us
  transfers between devices with their start and end apart: 13, of which 8 were waited for; matrix products, arithmetic and copies ran while one was open for 1% of the time, Pallas kernels for 5%

profile of v2, /device:TPU:0, one launch (start us, length us, event | category | flops | bytes accessed | tf_op | source)
XLA Modules:
  0.0 60.3 jit_solution(9650441889358231710)
XLA Ops:
  0.6 0.0 copy-start.1
  0.6 0.0 copy-start.2
  0.7 0.0 copy-start
  0.7 1.7 %shard_map.85 = (bf16[520,256]{1,0:T(8,128)(2,1)S(1)}, bf16[520,256]{1,0:T(8,128)(2,1)S(1)}, bf16[520,256]{1,0:T(8,128)(2,1)S(1)}, bf16[520,256]{1,0:T(8,128)(2,...) custom-call(s32[16]{0:T(128)} %tags_hbm.1, ...), custom_call_target="tpu_custom_call" | custom-call | bytes 2097152 | tf_op jit(solution)/shard_map/pallas_call | solution.py:98
  2.4 0.0 copy-start.3
  2.4 3.0 %collective-permute-start.3 = (bf16[520,256]{1,0:T(8,128)(2,1)S(1)}, bf16[520,256]{1,0:T(8,128)(2,1)S(1)}, u32[]{:S(2)}, u32[]{:S(2)}) collective-permute-start(bf16[520,256]{1,0:T(8,128)(2,1)S(1)} %get-tuple-element.24), channel_id=1, source_target_pairs={{0,4},{4,0},{8,12},{12,8},{16,20},{20,16},{24,28},{28,24},{1,5},{5... | collective-permute-start | bytes 798728 | tf_op jit(solution)/shard_map/ppermute | solution.py:362
  5.5 1.6 %collective-permute-start.4 = (bf16[520,256]{1,0:T(8,128)(2,1)S(1)}, bf16[520,256]{1,0:T(8,128)(2,1)S(1)}, u32[]{:S(2)}, u32[]{:S(2)}) collective-permute-start(bf16[520,256]{1,0:T(8,128)(2,1)S(1)} %get-tuple-element.25), channel_id=1, source_target_pairs={{0,8},{4,12},{8,0},{12,4},{16,24},{20,28},{24,16},{28,20},{1,9},{5... | collective-permute-start | bytes 798728 | tf_op jit(solution)/shard_map/ppermute | solution.py:362
  7.0 0.0 copy-done.1
  7.0 0.0 collective-permute-start.6
  7.0 1.9 %collective-permute-start = (bf16[520,256]{1,0:T(8,128)(2,1)S(1)}, bf16[520,256]{1,0:T(8,128)(2,1)S(1)}, u32[]{:S(2)}, u32[]{:S(2)}) collective-permute-start(bf16[520,256]{1,0:T(8,128)(2,1)S(1)} %get-tuple-element.19), channel_id=1, source_target_pairs={{0,4},{4,0},{8,12},{12,8},{16,20},{20,16},{24,28},{28,24},{1,5},{5... | collective-permute-start | bytes 798728 | tf_op jit(solution)/shard_map/ppermute | solution.py:362
  9.0 1.6 %collective-permute-start.1 = (bf16[520,256]{1,0:T(8,128)(2,1)S(1)}, bf16[520,256]{1,0:T(8,128)(2,1)S(1)}, u32[]{:S(2)}, u32[]{:S(2)}) collective-permute-start(bf16[520,256]{1,0:T(8,128)(2,1)S(1)} %get-tuple-element.20), channel_id=1, source_target_pairs={{0,8},{4,12},{8,0},{12,4},{16,24},{20,28},{24,16},{28,20},{1,9},{5... | collective-permute-start | bytes 798728 | tf_op jit(solution)/shard_map/ppermute | solution.py:362
  10.5 5.5 %collective-permute-done.6.refs_0_ = bf16[2,16,1280]{2,1,0:T(8,128)(2,1)S(1)} collective-permute-done((bf16[2,16,1280]{2,1,0:T(8,128)(2,1)S(1)}, bf16[2,16,1280]{2,1,0:T(8,128)(2,1)S(1)}, u32[]{:S(2)}, u32[]{:S(2)}) %collective-permute-start.6) | collective-permute-done | bytes 81952 | tf_op jit(solution)/shard_map/ppermute | solution.py:362
  16.0 5.0 %collective-permute-start.7 = (bf16[2,16,1280]{2,1,0:T(8,128)(2,1)S(1)}, bf16[2,16,1280]{2,1,0:T(8,128)(2,1)S(1)}, u32[]{:S(2)}, u32[]{:S(2)}) collective-permute-start(bf16[2,16,1280]{2,1,0:T(8,128)(2,1)S(1)} %copy-done.1), channel_id=1, source_target_pairs={{28,0},{24,4},{20,8},{16,12},{12,16},{8,20},{4,24},{0,28},{29,1},{... | collective-permute-start | bytes 245768 | tf_op jit(solution)/shard_map/ppermute | solution.py:368
  21.0 3.5 %collective-permute-done.7.refs_1_ = bf16[2,16,1280]{2,1,0:T(8,128)(2,1)S(1)} collective-permute-done((bf16[2,16,1280]{2,1,0:T(8,128)(2,1)S(1)}, bf16[2,16,1280]{2,1,0:T(8,128)(2,1)S(1)}, u32[]{:S(2)}, u32[]{:S(2)}) %collective-permute-start.7) | collective-permute-done | bytes 81952 | tf_op jit(solution)/shard_map/ppermute | solution.py:368
  24.5 0.0 collective-permute-start.2
  24.5 1.0 %shard_map.88 = (bf16[336,128]{1,0:T(8,128)(2,1)S(1)}, bf16[336,128]{1,0:T(8,128)(2,1)S(1)}) custom-call(bf16[2,16,1280]{2,1,0:T(8,128)(2,1)S(1)} %collective-permute-done.6.refs_0_, bf16[2,16,1280]{2,1,0:T(8,128)(2,1)S(1)} %collective-permute-done.7.refs_1_, bf16[1032,256]{1,0:T(8,128)(2,1)S(1)} %get-tuple-element.26.refs_2_), custom_call_target="tpu_custom_call" | custom-call | flops 83886080 | bytes 1048576 | tf_op jit(solution)/shard_map/pallas_call | solution.py:209
  25.6 4.9 %collective-permute-done.2.refs_0_ = bf16[2,16,1280]{2,1,0:T(8,128)(2,1)S(1)} collective-permute-done((bf16[2,16,1280]{2,1,0:T(8,128)(2,1)S(1)}, bf16[2,16,1280]{2,1,0:T(8,128)(2,1)S(1)}, u32[]{:S(2)}, u32[]{:S(2)}) %collective-permute-start.2) | collective-permute-done | bytes 81952 | tf_op jit(solution)/shard_map/ppermute | solution.py:359
  30.5 0.7 %collective-permute-start.8 = (bf16[336,128]{1,0:T(8,128)(2,1)S(1)}, bf16[336,128]{1,0:T(8,128)(2,1)S(1)}, u32[]{:S(2)}, u32[]{:S(2)}) collective-permute-start(bf16[336,128]{1,0:T(8,128)(2,1)S(1)} %get-tuple-element.27), channel_id=1, source_target_pairs={{0,12},{4,8},{8,4},{12,0},{16,28},{20,24},{24,20},{28,16},{1,13},{... | collective-permute-start | bytes 258056 | tf_op jit(solution)/shard_map/ppermute | solution.py:362
  31.2 0.0 collective-permute-done.3.refs_2_
  31.2 2.4 %collective-permute-start.9 = (bf16[336,128]{1,0:T(8,128)(2,1)S(1)}, bf16[336,128]{1,0:T(8,128)(2,1)S(1)}, u32[]{:S(2)}, u32[]{:S(2)}) collective-permute-start(bf16[336,128]{1,0:T(8,128)(2,1)S(1)} %get-tuple-element.28), channel_id=1, source_target_pairs={{28,0},{24,4},{20,8},{16,12},{12,16},{8,20},{4,24},{0,28},{29,1},{... | collective-permute-start | bytes 258056 | tf_op jit(solution)/shard_map/ppermute | solution.py:368
  33.6 0.0 collective-permute-done.4.refs_3_
  33.6 1.0 %shard_map.87 = bf16[336,128]{1,0:T(8,128)(2,1)S(1)} custom-call(bf16[2,16,1280]{2,1,0:T(8,128)(2,1)S(1)} %collective-permute-done.2.refs_0_, bf16[520,256]{1,0:T(8,128)(2,1)S(1)} %get-tuple-element.23.refs_1_, bf16[520,256]{1,0:T(8,128)(2,1)S(1)} %collective-permute-done.3.refs_2_, bf16[520,256]{1,0:T(8,128)(2,1)S(1)} %collective-permute-done.4.refs_3_), custom_call_target="tpu_custom_call" | custom-call | flops 125829120 | bytes 1048576 | tf_op jit(solution)/shard_map/pallas_call | solution.py:209
  34.6 1.4 %collective-permute-start.5 = (bf16[336,128]{1,0:T(8,128)(2,1)S(1)}, bf16[336,128]{1,0:T(8,128)(2,1)S(1)}, u32[]{:S(2)}, u32[]{:S(2)}) collective-permute-start(bf16[336,128]{1,0:T(8,128)(2,1)S(1)} %shard_map.87), channel_id=1, source_target_pairs={{16,0},{20,4},{24,8},{28,12},{0,16},{4,20},{8,24},{12,28},{17,1},{... | collective-permute-start | bytes 258056 | tf_op jit(solution)/shard_map/ppermute | solution.py:359
  36.0 0.0 collective-permute-done.refs_3_
  36.0 0.0 collective-permute-done.1.refs_4_
  36.0 0.0 copy-done.2
  36.0 1.1 %shard_map.86 = (f32[320,128]{1,0:T(8,128)S(1)}, f32[320,128]{1,0:T(8,128)S(1)}) custom-call(bf16[2,16,1280]{2,1,0:T(8,128)(2,1)S(1)} %copy-done.1, bf16[2,2,16,256]{3,2,1,0:T(8,128)(2,1)S(1)} %copy-done.2, bf16[520,256]{1,0:T(8,128)(2,1)S(1)} %get-tuple-element.18.refs_2_, bf16[520,256]{1,0:T(8,128)(2,1)S(1)} %collective-permute-done.refs_3_, ...), custom_call_target="tpu_custom_call" | custom-call | flops 125829120 | bytes 1048576 | tf_op jit(solution)/shard_map/pallas_call | solution.py:249
  37.1 0.0 collective-permute-done.8.refs_4_
  37.1 1.3 %collective-permute-done.9.refs_5_ = bf16[336,128]{1,0:T(8,128)(2,1)S(1)} collective-permute-done((bf16[336,128]{1,0:T(8,128)(2,1)S(1)}, bf16[336,128]{1,0:T(8,128)(2,1)S(1)}, u32[]{:S(2)}, u32[]{:S(2)}) %collective-permute-start.9) | collective-permute-done | bytes 86048 | tf_op jit(solution)/shard_map/ppermute | solution.py:368
  38.5 2.5 %collective-permute-done.5.refs_3_ = bf16[336,128]{1,0:T(8,128)(2,1)S(1)} collective-permute-done((bf16[336,128]{1,0:T(8,128)(2,1)S(1)}, bf16[336,128]{1,0:T(8,128)(2,1)S(1)}, u32[]{:S(2)}, u32[]{:S(2)}) %collective-permute-start.5) | collective-permute-done | bytes 86048 | tf_op jit(solution)/shard_map/ppermute | solution.py:359
  41.0 0.0 copy-done
  41.0 1.1 %shard_map.89 = (bf16[2,16,1280]{2,1,0:T(8,128)(2,1)}, f32[32,128]{1,0:T(8,128)S(1)}) custom-call(f32[320,128]{1,0:T(8,128)S(1)} %get-tuple-element.21.refs_0_, f32[320,128]{1,0:T(8,128)S(1)} %get-tuple-element.22.refs_1_, bf16[1280,128]{1,0:T(8,128)(2,1)S(1)} %copy-done, bf16[336,128]{1,0:T(8,128)(2,1)S(1)} %collective-permute-done.5.refs_3_, ...), custom_call_target="tpu_custom_call" | custom-call | flops 16777216 | bytes 1048576 | tf_op jit(solution)/shard_map/pallas_call | solution.py:300
  42.1 5.2 %all-gather = f32[128,128]{1,0:T(8,128)S(1)} all-gather(f32[32,128]{1,0:T(8,128)S(1)} %get-tuple-element.30), channel_id=2, replica_groups=mesh['dp'=8,'mp'=4] {'mp'}, dimensions={0}, use_global_device_ids=true | all-gather | bytes 81920 | tf_op jit(solution)/shard_map/all_gather | solution.py:390
  47.3 0.0 copy-done.3
  47.3 0.7 %shard_map.90 = (f32[2,128]{1,0:T(2,128)S(1)}, f32[1,128]{1,0:T(1,128)S(1)}) custom-call(s32[2]{0:T(128)S(1)} %copy-done.3, f32[4,32,128]{2,1,0:T(8,128)S(1)} %bitcast.2), custom_call_target="tpu_custom_call" | custom-call | flops 1048576 | bytes 65536 | tf_op jit(solution)/shard_map/pallas_call | solution.py:337
  48.0 0.1 collective-permute-start.10
  48.1 3.6 %collective-permute-done.10 = f32[1,128]{1,0:T(1,128)S(1)} collective-permute-done((f32[1,128]{1,0:T(1,128)S(1)}, f32[1,128]{1,0:T(1,128)S(1)}, u32[]{:S(2)}, u32[]{:S(2)}) %collective-permute-start.10) | collective-permute-done | bytes 544 | tf_op jit(solution)/shard_map/ppermute | solution.py:362
  51.7 0.2 collective-permute-start.11
  51.8 3.4 %collective-permute-done.11 = f32[1,128]{1,0:T(1,128)S(1)} collective-permute-done((f32[1,128]{1,0:T(1,128)S(1)}, f32[1,128]{1,0:T(1,128)S(1)}, u32[]{:S(2)}, u32[]{:S(2)}) %collective-permute-start.11) | collective-permute-done | bytes 544 | tf_op jit(solution)/shard_map/ppermute | solution.py:362
  55.2 0.5 collective-permute-start.12
  55.7 0.6 %slice_reduce_fusion = f32[2]{0:T(128)} fusion(f32[2,128]{1,0:T(2,128)S(1)} %get-tuple-element.31), kind=kLoop, calls=%fused_computation | loop fusion | bytes 16 | tf_op jit(solution)/shard_map/slice | solution.py:393
  56.4 3.3 %collective-permute-done.12 = f32[1,128]{1,0:T(1,128)S(1)} collective-permute-done((f32[1,128]{1,0:T(1,128)S(1)}, f32[1,128]{1,0:T(1,128)S(1)}, u32[]{:S(2)}, u32[]{:S(2)}) %collective-permute-start.12) | collective-permute-done | bytes 544 | tf_op jit(solution)/shard_map/ppermute | solution.py:362
  59.7 0.6 constant_dynamic-slice_fusion
  (3 shorter events, 0.0 us)
Async XLA Ops:
  0.6 6.4 %copy-start.1 = (bf16[2,16,1280]{2,1,0:T(8,128)(2,1)S(1)}, bf16[2,16,1280]{2,1,0:T(8,128)(2,1)}, u32[]{:S(2)}) copy-start(bf16[2,16,1280]{2,1,0:T(8,128)(2,1)} %refs_0_.1) | copy-start | bytes 245764
  0.6 35.4 %copy-start.2 = (bf16[2,2,16,256]{3,2,1,0:T(8,128)(2,1)S(1)}, bf16[2,2,16,256]{3,2,1,0:T(8,128)(2,1)}, u32[]{:S(2)}) copy-start(bf16[2,2,16,256]{3,2,1,0:T(8,128)(2,1)} %refs_1_.1) | copy-start | bytes 98308
  0.7 40.3 %copy-start = (bf16[1280,128]{1,0:T(8,128)(2,1)S(1)}, bf16[1280,128]{1,0:T(8,128)(2,1)}, u32[]{:S(2)}) copy-start(bf16[1280,128]{1,0:T(8,128)(2,1)} %refs_2_.1) | copy-start | bytes 983044
  2.4 44.9 %copy-start.3 = (s32[2]{0:T(128)S(1)}, s32[2]{0:T(128)}, u32[]{:S(2)}) copy-start(s32[2]{0:T(128)} %answer_ref.1) | copy-start | bytes 28
  2.4 28.7 %collective-permute-start.3 = (bf16[520,256]{1,0:T(8,128)(2,1)S(1)}, bf16[520,256]{1,0:T(8,128)(2,1)S(1)}, u32[]{:S(2)}, u32[]{:S(2)}) collective-permute-start(bf16[520,256]{1,0:T(8,128)(2,1)S(1)} %get-tuple-element.24), channel_id=1, source_target_pairs={{0,4},{4,0},{8,12},{12,8},{16,20},{20,16},{24,28},{28,24},{1,5},{5... | collective-permute-start | bytes 798728 | tf_op jit(solution)/shard_map/ppermute | solution.py:362
  5.5 28.1 %collective-permute-start.4 = (bf16[520,256]{1,0:T(8,128)(2,1)S(1)}, bf16[520,256]{1,0:T(8,128)(2,1)S(1)}, u32[]{:S(2)}, u32[]{:S(2)}) collective-permute-start(bf16[520,256]{1,0:T(8,128)(2,1)S(1)} %get-tuple-element.25), channel_id=1, source_target_pairs={{0,8},{4,12},{8,0},{12,4},{16,24},{20,28},{24,16},{28,20},{1,9},{5... | collective-permute-start | bytes 798728 | tf_op jit(solution)/shard_map/ppermute | solution.py:362
  7.0 9.0 %collective-permute-start.6 = (bf16[2,16,1280]{2,1,0:T(8,128)(2,1)S(1)}, bf16[2,16,1280]{2,1,0:T(8,128)(2,1)S(1)}, u32[]{:S(2)}, u32[]{:S(2)}) collective-permute-start(bf16[2,16,1280]{2,1,0:T(8,128)(2,1)S(1)} %copy-done.1), channel_id=1, source_target_pairs={{0,12},{4,8},{8,4},{12,0},{16,28},{20,24},{24,20},{28,16},{1,13},{... | collective-permute-start | bytes 245768 | tf_op jit(solution)/shard_map/ppermute | solution.py:362
  7.0 29.0 %collective-permute-start = (bf16[520,256]{1,0:T(8,128)(2,1)S(1)}, bf16[520,256]{1,0:T(8,128)(2,1)S(1)}, u32[]{:S(2)}, u32[]{:S(2)}) collective-permute-start(bf16[520,256]{1,0:T(8,128)(2,1)S(1)} %get-tuple-element.19), channel_id=1, source_target_pairs={{0,4},{4,0},{8,12},{12,8},{16,20},{20,16},{24,28},{28,24},{1,5},{5... | collective-permute-start | bytes 798728 | tf_op jit(solution)/shard_map/ppermute | solution.py:362
  9.0 27.1 %collective-permute-start.1 = (bf16[520,256]{1,0:T(8,128)(2,1)S(1)}, bf16[520,256]{1,0:T(8,128)(2,1)S(1)}, u32[]{:S(2)}, u32[]{:S(2)}) collective-permute-start(bf16[520,256]{1,0:T(8,128)(2,1)S(1)} %get-tuple-element.20), channel_id=1, source_target_pairs={{0,8},{4,12},{8,0},{12,4},{16,24},{20,28},{24,16},{28,20},{1,9},{5... | collective-permute-start | bytes 798728 | tf_op jit(solution)/shard_map/ppermute | solution.py:362
  16.0 8.5 %collective-permute-start.7 = (bf16[2,16,1280]{2,1,0:T(8,128)(2,1)S(1)}, bf16[2,16,1280]{2,1,0:T(8,128)(2,1)S(1)}, u32[]{:S(2)}, u32[]{:S(2)}) collective-permute-start(bf16[2,16,1280]{2,1,0:T(8,128)(2,1)S(1)} %copy-done.1), channel_id=1, source_target_pairs={{28,0},{24,4},{20,8},{16,12},{12,16},{8,20},{4,24},{0,28},{29,1},{... | collective-permute-start | bytes 245768 | tf_op jit(solution)/shard_map/ppermute | solution.py:368
  24.5 6.0 %collective-permute-start.2 = (bf16[2,16,1280]{2,1,0:T(8,128)(2,1)S(1)}, bf16[2,16,1280]{2,1,0:T(8,128)(2,1)S(1)}, u32[]{:S(2)}, u32[]{:S(2)}) collective-permute-start(bf16[2,16,1280]{2,1,0:T(8,128)(2,1)S(1)} %copy-done.1), channel_id=1, source_target_pairs={{16,0},{20,4},{24,8},{28,12},{0,16},{4,20},{8,24},{12,28},{17,1},{... | collective-permute-start | bytes 245768 | tf_op jit(solution)/shard_map/ppermute | solution.py:359
  30.5 6.6 %collective-permute-start.8 = (bf16[336,128]{1,0:T(8,128)(2,1)S(1)}, bf16[336,128]{1,0:T(8,128)(2,1)S(1)}, u32[]{:S(2)}, u32[]{:S(2)}) collective-permute-start(bf16[336,128]{1,0:T(8,128)(2,1)S(1)} %get-tuple-element.27), channel_id=1, source_target_pairs={{0,12},{4,8},{8,4},{12,0},{16,28},{20,24},{24,20},{28,16},{1,13},{... | collective-permute-start | bytes 258056 | tf_op jit(solution)/shard_map/ppermute | solution.py:362
  31.2 7.3 %collective-permute-start.9 = (bf16[336,128]{1,0:T(8,128)(2,1)S(1)}, bf16[336,128]{1,0:T(8,128)(2,1)S(1)}, u32[]{:S(2)}, u32[]{:S(2)}) collective-permute-start(bf16[336,128]{1,0:T(8,128)(2,1)S(1)} %get-tuple-element.28), channel_id=1, source_target_pairs={{28,0},{24,4},{20,8},{16,12},{12,16},{8,20},{4,24},{0,28},{29,1},{... | collective-permute-start | bytes 258056 | tf_op jit(solution)/shard_map/ppermute | solution.py:368
  34.6 6.4 %collective-permute-start.5 = (bf16[336,128]{1,0:T(8,128)(2,1)S(1)}, bf16[336,128]{1,0:T(8,128)(2,1)S(1)}, u32[]{:S(2)}, u32[]{:S(2)}) collective-permute-start(bf16[336,128]{1,0:T(8,128)(2,1)S(1)} %shard_map.87), channel_id=1, source_target_pairs={{16,0},{20,4},{24,8},{28,12},{0,16},{4,20},{8,24},{12,28},{17,1},{... | collective-permute-start | bytes 258056 | tf_op jit(solution)/shard_map/ppermute | solution.py:359
  48.0 3.6 %collective-permute-start.10 = (f32[1,128]{1,0:T(1,128)S(1)}, f32[1,128]{1,0:T(1,128)S(1)}, u32[]{:S(2)}, u32[]{:S(2)}) collective-permute-start(f32[1,128]{1,0:T(1,128)S(1)} %get-tuple-element.32), channel_id=1, source_target_pairs={{0,4},{4,0},{8,12},{12,8},{16,20},{20,16},{24,28},{28,24},{1,5},{5... | collective-permute-start | bytes 1544 | tf_op jit(solution)/shard_map/ppermute | solution.py:362
  51.7 3.6 %collective-permute-start.11 = (f32[1,128]{1,0:T(1,128)S(1)}, f32[1,128]{1,0:T(1,128)S(1)}, u32[]{:S(2)}, u32[]{:S(2)}) collective-permute-start(f32[1,128]{1,0:T(1,128)S(1)} %add.12), channel_id=1, source_target_pairs={{0,8},{4,12},{8,0},{12,4},{16,24},{20,28},{24,16},{28,20},{1,9},{5... | collective-permute-start | bytes 1544 | tf_op jit(solution)/shard_map/ppermute | solution.py:362
  55.2 4.5 %collective-permute-start.12 = (f32[1,128]{1,0:T(1,128)S(1)}, f32[1,128]{1,0:T(1,128)S(1)}, u32[]{:S(2)}, u32[]{:S(2)}) collective-permute-start(f32[1,128]{1,0:T(1,128)S(1)} %add.13), channel_id=1, source_target_pairs={{0,16},{4,20},{8,24},{12,28},{16,0},{20,4},{24,8},{28,12},{1,17},{... | collective-permute-start | bytes 1544 | tf_op jit(solution)/shard_map/ppermute | solution.py:362
